TPU v7x, 512 devices: a 4x2x32 block of a 4x8x32 slice. The times are simulated.
512 devices in a mesh: ens: 2 (over y), gx: 32 (over z), col: 4 (over x), gz: 2 (over core).
Axes of the slice: x: 4, y: 2, z: 32, core: 2. Of those that a mesh axis runs over, the one named last changes fastest.
The devices are a block of a 4x8x32 slice.
Arguments:
- checkpoints: bfloat16 [8, 3, 32, 64, 512], P(('ens', 'col'), None, 'gz', 'gx'), parts along dimension 0, may hold values from -3 to 3
- obs_values: float32 [8, 32, 64, 512], P('ens', 'gz', 'gx', 'col'), parts along dimension 0, may hold values from -3 to 3
- obs_mask: int32 [8, 32, 64, 512], P('ens', 'gz', 'gx', 'col'), parts along dimension 0, may hold values 0 or 1
- drag: float32 [64], P(('ens', 'gz')), parts along dimension 0, may hold values from 0.05 to 0.5
Outputs:
- grad_init: float32 [6, 32, 64, 512], P('ens', 'gz', 'gx', 'col'), parts along dimension 0
- cost_levels: float32 [64], P(('ens', 'gz')), parts along dimension 0
- drag_grad: float32 [64], P(('ens', 'gz')), parts along dimension 0
There are 2 independent parts, one for each index of `ens`. A program takes and returns all parts, laid end to end along the dimension named above; each array names one. Nothing has to cross between parts.
All inputs are finite; a program needn't handle non-finite values. No bound on the sum of `obs_mask` on one device may be relied on, other than what follows from the above.
Results may differ from a plain program's by a relative error of at most 0.0003.
Values may be sent and summed in bfloat16 or wider, within the bound.
No kernel may reach another device: no remote copies, remote signals or barrier semaphores. Data moves between devices by JAX's collectives and lax.ppermute only.
A program may use at most 64 MiB of HBM per device.

v0:
```python
import functools

import jax
import jax.numpy as jnp
from jax import lax
from jax.sharding import PartitionSpec as P

SEG = 2


time_step = 0.1
viscosity = 0.05
vertical_mix = 0.2


def padded_2(x, sides, width):
    edges = {}
    for axis, dim in sides:
        devices, length = (lax.axis_size(axis), x.shape[dim])
        up = [(i, (i + 1) % devices) for i in range(devices - 1)]
        last = lax.slice_in_dim(x, length - width, length, axis=dim)
        initial = lax.slice_in_dim(x, 0, width, axis=dim)
        edges[dim] = (
            lax.ppermute(last, axis, up),
            lax.ppermute(initial, axis, [(b, a) for a, b in up]),
        )
    done = []
    for _, dim in sides:
        low, high = edges[dim]
        around = [(width, width) if d in done else (0, 0) for d in range(x.ndim)]
        x = jnp.concatenate([jnp.pad(low, around), x, jnp.pad(high, around)], axis=dim)
        done.append(dim)
    return x


def passed_along(block, axis, distance):
    devices = range(lax.axis_size(axis))
    route = [(i - distance, i) for i in devices if i - distance in devices]
    return lax.ppermute(block, axis, route)


def by_axis(x, axes):
    return functools.reduce(lax.psum, axes, x)


def along_cols(a):
    return 0.5 * (a[:, 1:-1, 2:] - a[:, 1:-1, :-2])


def along_rows(a):
    return 0.5 * (a[:, 2:, 1:-1] - a[:, :-2, 1:-1])


def laplace(a):
    return (
        a[:, 2:, 1:-1] + a[:, :-2, 1:-1] + a[:, 1:-1, 2:] + a[:, 1:-1, :-2] - 4.0 * a[:, 1:-1, 1:-1]
    )


def advance(padded, drag, coriolis):
    levels = padded[:, 1:-1]
    thick, zonal, merid = (levels[0], levels[1], levels[2])
    centre = padded[:, 1:-1, 1:-1, 1:-1]
    h_c, u_c, v_c = (centre[0], centre[1], centre[2])
    rot = coriolis[None, :, None]
    rate = drag[:, None, None]
    vert = padded[:, 2:, 1:-1, 1:-1] + padded[:, :-2, 1:-1, 1:-1] - 2.0 * centre
    u_new = (
        u_c
        + time_step
        * (
            -along_cols(thick)
            - u_c * along_cols(zonal)
            - v_c * along_rows(zonal)
            + rot * v_c
            - rate * u_c
        )
        + viscosity * laplace(zonal)
    )
    v_new = (
        v_c
        + time_step
        * (
            -along_rows(thick)
            - u_c * along_cols(merid)
            - v_c * along_rows(merid)
            - rot * u_c
            - rate * v_c
        )
        + viscosity * laplace(merid)
    )
    h_new = (
        h_c
        - time_step
        * (
            along_cols(zonal)
            + along_rows(merid)
            + along_cols(thick * zonal)
            + along_rows(thick * merid)
        )
        + viscosity * laplace(thick)
    )
    return jnp.stack([h_new, u_new, v_new]) + vertical_mix * vert


def extend(state):
    return padded_2(state, (("gx", 2), ("col", 3), ("gz", 1)), 1)


def halo_back(cot):
    inner = cot[:, 1:-1, 1:-1, 1:-1]
    below = passed_along(cot[:, 0, 1:-1, 1:-1], "gz", -1)
    above = passed_along(cot[:, -1, 1:-1, 1:-1], "gz", 1)
    inner = inner.at[:, -1].add(below).at[:, 0].add(above)
    south = passed_along(cot[:, 1:-1, 0, 1:-1], "gx", -1)
    north = passed_along(cot[:, 1:-1, -1, 1:-1], "gx", 1)
    inner = inner.at[:, :, -1].add(south).at[:, :, 0].add(north)
    west = passed_along(cot[:, 1:-1, 1:-1, 0], "col", -1)
    east = passed_along(cot[:, 1:-1, 1:-1, -1], "col", 1)
    return inner.at[:, :, :, -1].add(west).at[:, :, :, 0].add(east)


def on_device(checkpoints, obs_values, obs_mask, drag):
    lat_count = obs_values.shape[2]
    lon_count = obs_values.shape[3]
    segments = obs_values.shape[0]
    total_lat = lat_count * lax.axis_size("gx")
    total_lon = lon_count * lax.axis_size("col")
    rows = (lax.axis_index("gx") * lat_count + jnp.arange(lat_count)).astype(jnp.float32)
    cols = (lax.axis_index("col") * lon_count + jnp.arange(lon_count)).astype(jnp.float32)
    coriolis = 0.2 + 0.1 * rows / total_lat
    weight = (1.0 + 2.0 * rows / total_lat)[:, None] * (1.0 + 2.0 * cols / total_lon)[None, :]
    owned_cols = lax.all_to_all(checkpoints, "col", split_axis=4, concat_axis=0, tiled=True)

    def local(padded, rate):
        return advance(padded, rate, coriolis)

    levels = drag.shape[0]
    adjoint = jnp.zeros((3, levels, lat_count, lon_count), jnp.float32)
    cost = jnp.zeros((levels,), jnp.float32)
    drag_total = jnp.zeros((levels,), jnp.float32)
    for seg in reversed(range(segments)):
        state = owned_cols[seg].astype(jnp.float32)
        pads = []
        for step in range(SEG):
            padded = extend(state)
            pads.append(padded)
            state = advance(padded, drag, coriolis)
        resid = state[0] - obs_values[seg]
        forcing = weight[None] * obs_mask[seg].astype(jnp.float32) * resid
        seg_cost = 0.5 * jnp.sum(forcing * resid, axis=(1, 2))
        adjoint = adjoint.at[0].add(forcing)
        seg_drag = jnp.zeros((levels,), jnp.float32)
        for step in reversed(range(SEG)):
            unused, pull = jax.vjp(local, pads[step], drag)
            cot_pad, cot_drag = pull(adjoint)
            seg_drag = seg_drag + cot_drag
            adjoint = halo_back(cot_pad)
        summed_drag, summed_cost = (
            by_axis(seg_drag, ("gx", "col")),
            by_axis(seg_cost, ("gx", "col")),
        )
        drag_total = drag_total + summed_drag
        cost = cost + summed_cost
    scale = 1.0 / (total_lat * total_lon)
    return (adjoint, cost * scale, drag_total * scale)


def solution(mesh):
    return jax.shard_map(
        on_device,
        mesh=mesh,
        in_specs=(
            P(("ens", "col"), None, "gz", "gx", None),
            P("ens", "gz", "gx", "col"),
            P("ens", "gz", "gx", "col"),
            P(("ens", "gz")),
        ),
        out_specs=(P("ens", "gz", "gx", "col"), P(("ens", "gz")), P(("ens", "gz"))),
        check_vma=False,
    )
```

profile of v0, /device:TPU:40, one launch (start us, length us, event | category | flops | bytes accessed | tf_op | source)
XLA Modules:
  0.0 432.2 jit_solution(1579362360835207572)
XLA Ops:
  4.4 4.7 %all-to-all-start = ((bf16[4,2,6144]{2,1,0:T(2,128)(2,1)}), bf16[4,2,6144]{2,1,0:T(2,128)(2,1)S(1)}, u32[]{:S(2)}, u32[]{:S(2)}) async-start(bf16[4,2,6144]{2,1,0:T(2,128)(2,1)} %reshape.2013), calls=%async_computation | async-start | bytes 196608 | tf_op jit(solution)/shard_map/all_to_all | solution.py:133
  19.6 4.7 %collective-permute-start.1 = (f32[3,16,1,128]{3,1,2,0:T(8,128)S(1)}, f32[3,16,1,128]{3,1,2,0:T(8,128)S(1)}, u32[]{:S(2)}, u32[]{:S(2)}) collective-permute-start(f32[3,16,1,128]{3,1,2,0:T(8,128)S(1)} %get-tuple-element.1018), channel_id=1, source_target_pairs={{0,8},{8,16},{16,24},{24,32},{32,40},{40,48},{48,56},{56,64},{64,7... | collective-permute-start | bytes 73736 | tf_op jit(solution)/shard_map/ppermute | solution.py:24
  27.0 4.6 %collective-permute-start.24 = (f32[3,16,2,1]{3,1,2,0:T(8,128)S(1)}, f32[3,16,2,1]{3,1,2,0:T(8,128)S(1)}, u32[]{:S(2)}, u32[]{:S(2)}) collective-permute-start(f32[3,16,2,1]{3,1,2,0:T(8,128)S(1)} %get-tuple-element.1034), channel_id=1, source_target_pairs={{0,2},{2,4},{4,6},{1,3},{3,5},{5,7},{8,10},{10,12},{12,14},{9,11},... | collective-permute-start | bytes 1160 | tf_op jit(solution)/shard_map/ppermute | solution.py:24
  32.9 4.6 %collective-permute-start.48 = (f32[3,16,2,1]{3,1,2,0:T(8,128)S(1)}, f32[3,16,2,1]{3,1,2,0:T(8,128)S(1)}, u32[]{:S(2)}, u32[]{:S(2)}) collective-permute-start(f32[3,16,2,1]{3,1,2,0:T(8,128)S(1)} %get-tuple-element.1048), channel_id=1, source_target_pairs={{0,2},{2,4},{4,6},{1,3},{3,5},{5,7},{8,10},{10,12},{12,14},{9,11},... | collective-permute-start | bytes 1160 | tf_op jit(solution)/shard_map/ppermute | solution.py:24
  38.9 4.6 %collective-permute-start.72 = (f32[3,16,2,1]{3,1,2,0:T(8,128)S(1)}, f32[3,16,2,1]{3,1,2,0:T(8,128)S(1)}, u32[]{:S(2)}, u32[]{:S(2)}) collective-permute-start(f32[3,16,2,1]{3,1,2,0:T(8,128)S(1)} %get-tuple-element.1060), channel_id=1, source_target_pairs={{0,2},{2,4},{4,6},{1,3},{3,5},{5,7},{8,10},{10,12},{12,14},{9,11},... | collective-permute-start | bytes 1160 | tf_op jit(solution)/shard_map/ppermute | solution.py:24
  49.5 5.3 %collective-permute-start.25 = (f32[3,16,1,128]{3,1,2,0:T(8,128)S(1)}, f32[3,16,1,128]{3,1,2,0:T(8,128)S(1)}, u32[]{:S(2)}, u32[]{:S(2)}) collective-permute-start(f32[3,16,1,128]{3,1,2,0:T(8,128)S(1)} %get-tuple-element.1032), channel_id=1, source_target_pairs={{0,8},{8,16},{16,24},{24,32},{32,40},{40,48},{48,56},{56,64},{64,7... | collective-permute-start | bytes 73736 | tf_op jit(solution)/shard_map/ppermute | solution.py:24
  61.4 5.9 %collective-permute-start.49 = (f32[3,16,1,128]{3,1,2,0:T(8,128)S(1)}, f32[3,16,1,128]{3,1,2,0:T(8,128)S(1)}, u32[]{:S(2)}, u32[]{:S(2)}) collective-permute-start(f32[3,16,1,128]{3,1,2,0:T(8,128)S(1)} %get-tuple-element.1046), channel_id=1, source_target_pairs={{0,8},{8,16},{16,24},{24,32},{32,40},{40,48},{48,56},{56,64},{64,7... | collective-permute-start | bytes 73736 | tf_op jit(solution)/shard_map/ppermute | solution.py:24
  74.8 5.1 %collective-permute-start.73 = (f32[3,16,1,128]{3,1,2,0:T(8,128)S(1)}, f32[3,16,1,128]{3,1,2,0:T(8,128)S(1)}, u32[]{:S(2)}, u32[]{:S(2)}) collective-permute-start(f32[3,16,1,128]{3,1,2,0:T(8,128)S(1)} %get-tuple-element.1058), channel_id=1, source_target_pairs={{0,8},{8,16},{16,24},{24,32},{32,40},{40,48},{48,56},{56,64},{64,7... | collective-permute-start | bytes 73736 | tf_op jit(solution)/shard_map/ppermute | solution.py:24
  94.1 5.2 %collective-permute-start.7 = (f32[3,16,1,128]{3,1,2,0:T(8,128)S(1)}, f32[3,16,1,128]{3,1,2,0:T(8,128)S(1)}, u32[]{:S(2)}, u32[]{:S(2)}) collective-permute-start(f32[3,16,1,128]{3,1,2,0:T(8,128)S(1)} %get-tuple-element.1010), channel_id=1, source_target_pairs={{0,8},{8,16},{16,24},{24,32},{32,40},{40,48},{48,56},{56,64},{64,7... | collective-permute-start | bytes 73736 | tf_op jit(solution)/shard_map/ppermute | solution.py:24
  100.6 4.6 %collective-permute-start.30 = (f32[3,16,2,1]{3,1,2,0:T(8,128)S(1)}, f32[3,16,2,1]{3,1,2,0:T(8,128)S(1)}, u32[]{:S(2)}, u32[]{:S(2)}) collective-permute-start(f32[3,16,2,1]{3,1,2,0:T(8,128)S(1)} %get-tuple-element.1026), channel_id=1, source_target_pairs={{0,2},{2,4},{4,6},{1,3},{3,5},{5,7},{8,10},{10,12},{12,14},{9,11},... | collective-permute-start | bytes 1160 | tf_op jit(solution)/shard_map/ppermute | solution.py:24
  106.6 4.6 %collective-permute-start.54 = (f32[3,16,2,1]{3,1,2,0:T(8,128)S(1)}, f32[3,16,2,1]{3,1,2,0:T(8,128)S(1)}, u32[]{:S(2)}, u32[]{:S(2)}) collective-permute-start(f32[3,16,2,1]{3,1,2,0:T(8,128)S(1)} %get-tuple-element.1040), channel_id=1, source_target_pairs={{0,2},{2,4},{4,6},{1,3},{3,5},{5,7},{8,10},{10,12},{12,14},{9,11},... | collective-permute-start | bytes 1160 | tf_op jit(solution)/shard_map/ppermute | solution.py:24
  112.5 4.6 %collective-permute-start.78 = (f32[3,16,2,1]{3,1,2,0:T(8,128)S(1)}, f32[3,16,2,1]{3,1,2,0:T(8,128)S(1)}, u32[]{:S(2)}, u32[]{:S(2)}) collective-permute-start(f32[3,16,2,1]{3,1,2,0:T(8,128)S(1)} %get-tuple-element.1054), channel_id=1, source_target_pairs={{0,2},{2,4},{4,6},{1,3},{3,5},{5,7},{8,10},{10,12},{12,14},{9,11},... | collective-permute-start | bytes 1160 | tf_op jit(solution)/shard_map/ppermute | solution.py:24
  118.5 5.6 %collective-permute-start.31 = (f32[3,16,1,128]{3,1,2,0:T(8,128)S(1)}, f32[3,16,1,128]{3,1,2,0:T(8,128)S(1)}, u32[]{:S(2)}, u32[]{:S(2)}) collective-permute-start(f32[3,16,1,128]{3,1,2,0:T(8,128)S(1)} %get-tuple-element.1024), channel_id=1, source_target_pairs={{0,8},{8,16},{16,24},{24,32},{32,40},{40,48},{48,56},{56,64},{64,7... | collective-permute-start | bytes 73736 | tf_op jit(solution)/shard_map/ppermute | solution.py:24
  125.5 5.8 %collective-permute-start.55 = (f32[3,16,1,128]{3,1,2,0:T(8,128)S(1)}, f32[3,16,1,128]{3,1,2,0:T(8,128)S(1)}, u32[]{:S(2)}, u32[]{:S(2)}) collective-permute-start(f32[3,16,1,128]{3,1,2,0:T(8,128)S(1)} %get-tuple-element.1038), channel_id=1, source_target_pairs={{0,8},{8,16},{16,24},{24,32},{32,40},{40,48},{48,56},{56,64},{64,7... | collective-permute-start | bytes 73736 | tf_op jit(solution)/shard_map/ppermute | solution.py:24
  132.6 5.4 %collective-permute-start.79 = (f32[3,16,1,128]{3,1,2,0:T(8,128)S(1)}, f32[3,16,1,128]{3,1,2,0:T(8,128)S(1)}, u32[]{:S(2)}, u32[]{:S(2)}) collective-permute-start(f32[3,16,1,128]{3,1,2,0:T(8,128)S(1)} %get-tuple-element.1052), channel_id=1, source_target_pairs={{0,8},{8,16},{16,24},{24,32},{32,40},{40,48},{48,56},{56,64},{64,7... | collective-permute-start | bytes 73736 | tf_op jit(solution)/shard_map/ppermute | solution.py:24
  166.2 5.2 %collective-permute-start.17 = (f32[3,16,2]{1,2,0:T(2,128)S(1)}, f32[3,16,2]{1,2,0:T(2,128)S(1)}, u32[]{:S(2)}, u32[]{:S(2)}) collective-permute-start(f32[3,16,2]{1,2,0:T(2,128)S(1)} %get-tuple-element.654), channel_id=1, source_target_pairs={{0,2},{2,4},{4,6},{1,3},{3,5},{5,7},{8,10},{10,12},{12,14},{9,11},... | collective-permute-start | bytes 1160 | tf_op jit(solution)/shard_map/ppermute | solution.py:39
  174.5 6.4 %collective-permute-start.15 = (f32[3,16,128]{2,1,0:T(8,128)S(1)}, f32[3,16,128]{2,1,0:T(8,128)S(1)}, u32[]{:S(2)}, u32[]{:S(2)}) collective-permute-start(f32[3,16,128]{2,1,0:T(8,128)S(1)} %get-tuple-element.786), channel_id=1, source_target_pairs={{0,8},{8,16},{16,24},{24,32},{32,40},{40,48},{48,56},{56,64},{64,7... | collective-permute-start | bytes 73736 | tf_op jit(solution)/shard_map/ppermute | solution.py:39
  190.6 4.6 %collective-permute-start.23 = (f32[3,16,2]{1,2,0:T(2,128)S(1)}, f32[3,16,2]{1,2,0:T(2,128)S(1)}, u32[]{:S(2)}, u32[]{:S(2)}) collective-permute-start(f32[3,16,2]{1,2,0:T(2,128)S(1)} %bitcast.1246), channel_id=1, source_target_pairs={{0,2},{2,4},{4,6},{1,3},{3,5},{5,7},{8,10},{10,12},{12,14},{9,11},... | collective-permute-start | bytes 1160 | tf_op jit(solution)/shard_map/ppermute | solution.py:39
  196.5 5.8 %collective-permute-start.21 = (f32[3,16,128]{2,1,0:T(8,128)S(1)}, f32[3,16,128]{2,1,0:T(8,128)S(1)}, u32[]{:S(2)}, u32[]{:S(2)}) collective-permute-start(f32[3,16,128]{2,1,0:T(8,128)S(1)} %get-tuple-element.782), channel_id=1, source_target_pairs={{0,8},{8,16},{16,24},{24,32},{32,40},{40,48},{48,56},{56,64},{64,7... | collective-permute-start | bytes 73736 | tf_op jit(solution)/shard_map/ppermute | solution.py:39
  210.0 4.6 %collective-permute-start.41 = (f32[3,16,2]{1,2,0:T(2,128)S(1)}, f32[3,16,2]{1,2,0:T(2,128)S(1)}, u32[]{:S(2)}, u32[]{:S(2)}) collective-permute-start(f32[3,16,2]{1,2,0:T(2,128)S(1)} %get-tuple-element.652), channel_id=1, source_target_pairs={{0,2},{2,4},{4,6},{1,3},{3,5},{5,7},{8,10},{10,12},{12,14},{9,11},... | collective-permute-start | bytes 1160 | tf_op jit(solution)/shard_map/ppermute | solution.py:39
  217.1 5.8 %collective-permute-start.39 = (f32[3,16,128]{2,1,0:T(8,128)S(1)}, f32[3,16,128]{2,1,0:T(8,128)S(1)}, u32[]{:S(2)}, u32[]{:S(2)}) collective-permute-start(f32[3,16,128]{2,1,0:T(8,128)S(1)} %get-tuple-element.775), channel_id=1, source_target_pairs={{0,8},{8,16},{16,24},{24,32},{32,40},{40,48},{48,56},{56,64},{64,7... | collective-permute-start | bytes 73736 | tf_op jit(solution)/shard_map/ppermute | solution.py:39
  230.5 4.6 %collective-permute-start.47 = (f32[3,16,2]{1,2,0:T(2,128)S(1)}, f32[3,16,2]{1,2,0:T(2,128)S(1)}, u32[]{:S(2)}, u32[]{:S(2)}) collective-permute-start(f32[3,16,2]{1,2,0:T(2,128)S(1)} %get-tuple-element.650), channel_id=1, source_target_pairs={{0,2},{2,4},{4,6},{1,3},{3,5},{5,7},{8,10},{10,12},{12,14},{9,11},... | collective-permute-start | bytes 1160 | tf_op jit(solution)/shard_map/ppermute | solution.py:39
  237.6 5.8 %collective-permute-start.45 = (f32[3,16,128]{2,1,0:T(8,128)S(1)}, f32[3,16,128]{2,1,0:T(8,128)S(1)}, u32[]{:S(2)}, u32[]{:S(2)}) collective-permute-start(f32[3,16,128]{2,1,0:T(8,128)S(1)} %get-tuple-element.770), channel_id=1, source_target_pairs={{0,8},{8,16},{16,24},{24,32},{32,40},{40,48},{48,56},{56,64},{64,7... | collective-permute-start | bytes 73736 | tf_op jit(solution)/shard_map/ppermute | solution.py:39
  251.1 4.6 %collective-permute-start.65 = (f32[3,16,2]{1,2,0:T(2,128)S(1)}, f32[3,16,2]{1,2,0:T(2,128)S(1)}, u32[]{:S(2)}, u32[]{:S(2)}) collective-permute-start(f32[3,16,2]{1,2,0:T(2,128)S(1)} %get-tuple-element.648), channel_id=1, source_target_pairs={{0,2},{2,4},{4,6},{1,3},{3,5},{5,7},{8,10},{10,12},{12,14},{9,11},... | collective-permute-start | bytes 1160 | tf_op jit(solution)/shard_map/ppermute | solution.py:39
  258.2 6.1 %collective-permute-start.63 = (f32[3,16,128]{2,1,0:T(8,128)S(1)}, f32[3,16,128]{2,1,0:T(8,128)S(1)}, u32[]{:S(2)}, u32[]{:S(2)}) collective-permute-start(f32[3,16,128]{2,1,0:T(8,128)S(1)} %get-tuple-element.765), channel_id=1, source_target_pairs={{0,8},{8,16},{16,24},{24,32},{32,40},{40,48},{48,56},{56,64},{64,7... | collective-permute-start | bytes 73736 | tf_op jit(solution)/shard_map/ppermute | solution.py:39
  271.9 4.6 %collective-permute-start.71 = (f32[3,16,2]{1,2,0:T(2,128)S(1)}, f32[3,16,2]{1,2,0:T(2,128)S(1)}, u32[]{:S(2)}, u32[]{:S(2)}) collective-permute-start(f32[3,16,2]{1,2,0:T(2,128)S(1)} %get-tuple-element.646), channel_id=1, source_target_pairs={{0,2},{2,4},{4,6},{1,3},{3,5},{5,7},{8,10},{10,12},{12,14},{9,11},... | collective-permute-start | bytes 1160 | tf_op jit(solution)/shard_map/ppermute | solution.py:39
  279.0 6.1 %collective-permute-start.69 = (f32[3,16,128]{2,1,0:T(8,128)S(1)}, f32[3,16,128]{2,1,0:T(8,128)S(1)}, u32[]{:S(2)}, u32[]{:S(2)}) collective-permute-start(f32[3,16,128]{2,1,0:T(8,128)S(1)} %get-tuple-element.760), channel_id=1, source_target_pairs={{0,8},{8,16},{16,24},{24,32},{32,40},{40,48},{48,56},{56,64},{64,7... | collective-permute-start | bytes 73736 | tf_op jit(solution)/shard_map/ppermute | solution.py:39
  292.8 4.6 %collective-permute-start.89 = (f32[3,16,2]{1,2,0:T(2,128)S(1)}, f32[3,16,2]{1,2,0:T(2,128)S(1)}, u32[]{:S(2)}, u32[]{:S(2)}) collective-permute-start(f32[3,16,2]{1,2,0:T(2,128)S(1)} %get-tuple-element.644), channel_id=1, source_target_pairs={{0,2},{2,4},{4,6},{1,3},{3,5},{5,7},{8,10},{10,12},{12,14},{9,11},... | collective-permute-start | bytes 1160 | tf_op jit(solution)/shard_map/ppermute | solution.py:39
  299.9 6.1 %collective-permute-start.87 = (f32[3,16,128]{2,1,0:T(8,128)S(1)}, f32[3,16,128]{2,1,0:T(8,128)S(1)}, u32[]{:S(2)}, u32[]{:S(2)}) collective-permute-start(f32[3,16,128]{2,1,0:T(8,128)S(1)} %get-tuple-element.755), channel_id=1, source_target_pairs={{0,8},{8,16},{16,24},{24,32},{32,40},{40,48},{48,56},{56,64},{64,7... | collective-permute-start | bytes 73736 | tf_op jit(solution)/shard_map/ppermute | solution.py:39
  309.4 93.7 %all-reduce.344 = (f32[16]{0:T(128)S(1)}, f32[16]{0:T(128)S(1)}) all-reduce(f32[16]{0:T(128)S(1)} %add_multiply_fusion, f32[16]{0:T(128)S(1)} %add_add_fusion), channel_id=1, replica_groups=mesh['ens'=2,'gx'=32,'col'=4,'gz'=2] {'gx'}, use_global_device_ids=true, to_apply=%region_1.2 | all-reduce | flops 32 | bytes 256 | tf_op jit(solution)/shard_map/psum | solution.py:43
  403.1 9.5 %all-reduce.345 = (f32[16]{0:T(128)S(1)}, f32[16]{0:T(128)S(1)}) all-reduce(f32[16]{0:T(128)S(1)} %get-tuple-element.676, f32[16]{0:T(128)S(1)} %get-tuple-element.677), channel_id=1, replica_groups=mesh['ens'=2,'gx'=32,'col'=4,'gz'=2] {'col'}, use_global_device_ids=true, to_apply=%region_2.3 | all-reduce | flops 32 | bytes 256 | tf_op jit(solution)/shard_map/psum | solution.py:43
  417.9 4.6 %collective-permute-start.95 = (f32[3,16,2]{1,2,0:T(2,128)S(1)}, f32[3,16,2]{1,2,0:T(2,128)S(1)}, u32[]{:S(2)}, u32[]{:S(2)}) collective-permute-start(f32[3,16,2]{1,2,0:T(2,128)S(1)} %get-tuple-element.642), channel_id=1, source_target_pairs={{0,2},{2,4},{4,6},{1,3},{3,5},{5,7},{8,10},{10,12},{12,14},{9,11},... | collective-permute-start | bytes 1160 | tf_op jit(solution)/shard_map/ppermute | solution.py:39
  (525 shorter events, 170.3 us)
Async XLA Ops:
  17.1 14.5 %collective-permute-start = (f32[3,16,2,1]{3,1,2,0:T(8,128)S(1)}, f32[3,16,2,1]{3,1,2,0:T(8,128)S(1)}, u32[]{:S(2)}, u32[]{:S(2)}) collective-permute-start(f32[3,16,2,1]{3,1,2,0:T(8,128)S(1)} %get-tuple-element.1020), channel_id=1, source_target_pairs={{0,2},{2,4},{4,6},{1,3},{3,5},{5,7},{8,10},{10,12},{12,14},{9,11},... | collective-permute-start | bytes 1160 | tf_op jit(solution)/shard_map/ppermute | solution.py:24
  19.6 35.3 %collective-permute-start.1 = (f32[3,16,1,128]{3,1,2,0:T(8,128)S(1)}, f32[3,16,1,128]{3,1,2,0:T(8,128)S(1)}, u32[]{:S(2)}, u32[]{:S(2)}) collective-permute-start(f32[3,16,1,128]{3,1,2,0:T(8,128)S(1)} %get-tuple-element.1018), channel_id=1, source_target_pairs={{0,8},{8,16},{16,24},{24,32},{32,40},{40,48},{48,56},{56,64},{64,7... | collective-permute-start | bytes 73736 | tf_op jit(solution)/shard_map/ppermute | solution.py:24
  24.3 31.9 %collective-permute-start.2 = (f32[3,16,1,128]{3,1,2,0:T(8,128)S(1)}, f32[3,16,1,128]{3,1,2,0:T(8,128)S(1)}, u32[]{:S(2)}, u32[]{:S(2)}) collective-permute-start(f32[3,16,1,128]{3,1,2,0:T(8,128)S(1)} %get-tuple-element.1019), channel_id=1, source_target_pairs={{8,0},{16,8},{24,16},{32,24},{40,32},{48,40},{56,48},{64,56},{72,6... | collective-permute-start | bytes 73736 | tf_op jit(solution)/shard_map/ppermute | solution.py:25
  44.9 23.0 %collective-permute-start.4 = (f32[3,1,2,128]{3,1,2,0:T(1,128)S(1)}, f32[3,1,2,128]{3,1,2,0:T(1,128)S(1)}, u32[]{:S(2)}, u32[]{:S(2)}) collective-permute-start(f32[3,1,2,128]{3,1,2,0:T(1,128)S(1)} %get-tuple-element.1016), channel_id=1, source_target_pairs={{1,0},{3,2},{5,4},{7,6},{9,8},{11,10},{13,12},{15,14},{17,16},{19,... | collective-permute-start | bytes 9224 | tf_op jit(solution)/shard_map/ppermute | solution.py:25
  46.2 23.0 %collective-permute-start.5 = (f32[3,1,2,128]{3,1,2,0:T(1,128)S(1)}, f32[3,1,2,128]{3,1,2,0:T(1,128)S(1)}, u32[]{:S(2)}, u32[]{:S(2)}) collective-permute-start(f32[3,1,2,128]{3,1,2,0:T(1,128)S(1)} %get-tuple-element.1017), channel_id=1, source_target_pairs={{0,1},{2,3},{4,5},{6,7},{8,9},{10,11},{12,13},{14,15},{16,17},{18,... | collective-permute-start | bytes 9224 | tf_op jit(solution)/shard_map/ppermute | solution.py:24
  56.2 24.3 %collective-permute-start.28 = (f32[3,1,2,128]{3,1,2,0:T(1,128)S(1)}, f32[3,1,2,128]{3,1,2,0:T(1,128)S(1)}, u32[]{:S(2)}, u32[]{:S(2)}) collective-permute-start(f32[3,1,2,128]{3,1,2,0:T(1,128)S(1)} %get-tuple-element.1030), channel_id=1, source_target_pairs={{1,0},{3,2},{5,4},{7,6},{9,8},{11,10},{13,12},{15,14},{17,16},{19,... | collective-permute-start | bytes 9224 | tf_op jit(solution)/shard_map/ppermute | solution.py:25
  57.8 24.1 %collective-permute-start.29 = (f32[3,1,2,128]{3,1,2,0:T(1,128)S(1)}, f32[3,1,2,128]{3,1,2,0:T(1,128)S(1)}, u32[]{:S(2)}, u32[]{:S(2)}) collective-permute-start(f32[3,1,2,128]{3,1,2,0:T(1,128)S(1)} %get-tuple-element.1031), channel_id=1, source_target_pairs={{0,1},{2,3},{4,5},{6,7},{8,9},{10,11},{12,13},{14,15},{16,17},{18,... | collective-permute-start | bytes 9224 | tf_op jit(solution)/shard_map/ppermute | solution.py:24
  69.2 18.5 %collective-permute-start.52 = (f32[3,1,2,128]{3,1,2,0:T(1,128)S(1)}, f32[3,1,2,128]{3,1,2,0:T(1,128)S(1)}, u32[]{:S(2)}, u32[]{:S(2)}) collective-permute-start(f32[3,1,2,128]{3,1,2,0:T(1,128)S(1)} %get-tuple-element.1044), channel_id=1, source_target_pairs={{1,0},{3,2},{5,4},{7,6},{9,8},{11,10},{13,12},{15,14},{17,16},{19,... | collective-permute-start | bytes 9224 | tf_op jit(solution)/shard_map/ppermute | solution.py:25
  70.7 16.9 %collective-permute-start.53 = (f32[3,1,2,128]{3,1,2,0:T(1,128)S(1)}, f32[3,1,2,128]{3,1,2,0:T(1,128)S(1)}, u32[]{:S(2)}, u32[]{:S(2)}) collective-permute-start(f32[3,1,2,128]{3,1,2,0:T(1,128)S(1)} %get-tuple-element.1045), channel_id=1, source_target_pairs={{0,1},{2,3},{4,5},{6,7},{8,9},{10,11},{12,13},{14,15},{16,17},{18,... | collective-permute-start | bytes 9224 | tf_op jit(solution)/shard_map/ppermute | solution.py:24
  88.4 16.8 %collective-permute-start.6 = (f32[3,16,2,1]{3,1,2,0:T(8,128)S(1)}, f32[3,16,2,1]{3,1,2,0:T(8,128)S(1)}, u32[]{:S(2)}, u32[]{:S(2)}) collective-permute-start(f32[3,16,2,1]{3,1,2,0:T(8,128)S(1)} %get-tuple-element.1012), channel_id=1, source_target_pairs={{0,2},{2,4},{4,6},{1,3},{3,5},{5,7},{8,10},{10,12},{12,14},{9,11},... | collective-permute-start | bytes 1160 | tf_op jit(solution)/shard_map/ppermute | solution.py:24
  94.1 37.2 %collective-permute-start.7 = (f32[3,16,1,128]{3,1,2,0:T(8,128)S(1)}, f32[3,16,1,128]{3,1,2,0:T(8,128)S(1)}, u32[]{:S(2)}, u32[]{:S(2)}) collective-permute-start(f32[3,16,1,128]{3,1,2,0:T(8,128)S(1)} %get-tuple-element.1010), channel_id=1, source_target_pairs={{0,8},{8,16},{16,24},{24,32},{32,40},{40,48},{48,56},{56,64},{64,7... | collective-permute-start | bytes 73736 | tf_op jit(solution)/shard_map/ppermute | solution.py:24
  99.3 33.4 %collective-permute-start.8 = (f32[3,16,1,128]{3,1,2,0:T(8,128)S(1)}, f32[3,16,1,128]{3,1,2,0:T(8,128)S(1)}, u32[]{:S(2)}, u32[]{:S(2)}) collective-permute-start(f32[3,16,1,128]{3,1,2,0:T(8,128)S(1)} %get-tuple-element.1011), channel_id=1, source_target_pairs={{8,0},{16,8},{24,16},{32,24},{40,32},{48,40},{56,48},{64,56},{72,6... | collective-permute-start | bytes 73736 | tf_op jit(solution)/shard_map/ppermute | solution.py:25
  118.5 19.8 %collective-permute-start.31 = (f32[3,16,1,128]{3,1,2,0:T(8,128)S(1)}, f32[3,16,1,128]{3,1,2,0:T(8,128)S(1)}, u32[]{:S(2)}, u32[]{:S(2)}) collective-permute-start(f32[3,16,1,128]{3,1,2,0:T(8,128)S(1)} %get-tuple-element.1024), channel_id=1, source_target_pairs={{0,8},{8,16},{16,24},{24,32},{32,40},{40,48},{48,56},{56,64},{64,7... | collective-permute-start | bytes 73736 | tf_op jit(solution)/shard_map/ppermute | solution.py:24
  124.1 15.5 %collective-permute-start.32 = (f32[3,16,1,128]{3,1,2,0:T(8,128)S(1)}, f32[3,16,1,128]{3,1,2,0:T(8,128)S(1)}, u32[]{:S(2)}, u32[]{:S(2)}) collective-permute-start(f32[3,16,1,128]{3,1,2,0:T(8,128)S(1)} %get-tuple-element.1025), channel_id=1, source_target_pairs={{8,0},{16,8},{24,16},{32,24},{40,32},{48,40},{56,48},{64,56},{72,6... | collective-permute-start | bytes 73736 | tf_op jit(solution)/shard_map/ppermute | solution.py:25
  125.5 15.7 %collective-permute-start.55 = (f32[3,16,1,128]{3,1,2,0:T(8,128)S(1)}, f32[3,16,1,128]{3,1,2,0:T(8,128)S(1)}, u32[]{:S(2)}, u32[]{:S(2)}) collective-permute-start(f32[3,16,1,128]{3,1,2,0:T(8,128)S(1)} %get-tuple-element.1038), channel_id=1, source_target_pairs={{0,8},{8,16},{16,24},{24,32},{32,40},{40,48},{48,56},{56,64},{64,7... | collective-permute-start | bytes 73736 | tf_op jit(solution)/shard_map/ppermute | solution.py:24
  141.2 14.0 %collective-permute-start.35 = (f32[3,1,2,128]{3,1,2,0:T(1,128)S(1)}, f32[3,1,2,128]{3,1,2,0:T(1,128)S(1)}, u32[]{:S(2)}, u32[]{:S(2)}) collective-permute-start(f32[3,1,2,128]{3,1,2,0:T(1,128)S(1)} %get-tuple-element.1023), channel_id=1, source_target_pairs={{0,1},{2,3},{4,5},{6,7},{8,9},{10,11},{12,13},{14,15},{16,17},{18,... | collective-permute-start | bytes 9224 | tf_op jit(solution)/shard_map/ppermute | solution.py:24
  163.5 17.8 %collective-permute-start.14 = (f32[3,16,128]{2,1,0:T(8,128)S(1)}, f32[3,16,128]{2,1,0:T(8,128)S(1)}, u32[]{:S(2)}, u32[]{:S(2)}) collective-permute-start(f32[3,16,128]{2,1,0:T(8,128)S(1)} %get-tuple-element.787), channel_id=1, source_target_pairs={{8,0},{16,8},{24,16},{32,24},{40,32},{48,40},{56,48},{64,56},{72,6... | collective-permute-start | bytes 73736 | tf_op jit(solution)/shard_map/ppermute | solution.py:39
  164.8 16.3 %collective-permute-start.12 = (f32[3,2,128]{2,1,0:T(2,128)S(1)}, f32[3,2,128]{2,1,0:T(2,128)S(1)}, u32[]{:S(2)}, u32[]{:S(2)}) collective-permute-start(f32[3,2,128]{2,1,0:T(2,128)S(1)} %bitcast.1230), channel_id=1, source_target_pairs={{1,0},{3,2},{5,4},{7,6},{9,8},{11,10},{13,12},{15,14},{17,16},{19,... | collective-permute-start | bytes 9224 | tf_op jit(solution)/shard_map/ppermute | solution.py:39
  166.2 14.9 %collective-permute-start.17 = (f32[3,16,2]{1,2,0:T(2,128)S(1)}, f32[3,16,2]{1,2,0:T(2,128)S(1)}, u32[]{:S(2)}, u32[]{:S(2)}) collective-permute-start(f32[3,16,2]{1,2,0:T(2,128)S(1)} %get-tuple-element.654), channel_id=1, source_target_pairs={{0,2},{2,4},{4,6},{1,3},{3,5},{5,7},{8,10},{10,12},{12,14},{9,11},... | collective-permute-start | bytes 1160 | tf_op jit(solution)/shard_map/ppermute | solution.py:39
  184.5 18.1 %collective-permute-start.18 = (f32[3,2,128]{2,1,0:T(2,128)S(1)}, f32[3,2,128]{2,1,0:T(2,128)S(1)}, u32[]{:S(2)}, u32[]{:S(2)}) collective-permute-start(f32[3,2,128]{2,1,0:T(2,128)S(1)} %bitcast.1254), channel_id=1, source_target_pairs={{1,0},{3,2},{5,4},{7,6},{9,8},{11,10},{13,12},{15,14},{17,16},{19,... | collective-permute-start | bytes 9224 | tf_op jit(solution)/shard_map/ppermute | solution.py:39
  187.4 15.3 %collective-permute-start.19 = (f32[3,2,128]{2,1,0:T(2,128)S(1)}, f32[3,2,128]{2,1,0:T(2,128)S(1)}, u32[]{:S(2)}, u32[]{:S(2)}) collective-permute-start(f32[3,2,128]{2,1,0:T(2,128)S(1)} %bitcast.1255), channel_id=1, source_target_pairs={{0,1},{2,3},{4,5},{6,7},{8,9},{10,11},{12,13},{14,15},{16,17},{18,... | collective-permute-start | bytes 9224 | tf_op jit(solution)/shard_map/ppermute | solution.py:39
  205.8 17.4 %collective-permute-start.36 = (f32[3,2,128]{2,1,0:T(2,128)S(1)}, f32[3,2,128]{2,1,0:T(2,128)S(1)}, u32[]{:S(2)}, u32[]{:S(2)}) collective-permute-start(f32[3,2,128]{2,1,0:T(2,128)S(1)} %bitcast.1231), channel_id=1, source_target_pairs={{1,0},{3,2},{5,4},{7,6},{9,8},{11,10},{13,12},{15,14},{17,16},{19,... | collective-permute-start | bytes 9224 | tf_op jit(solution)/shard_map/ppermute | solution.py:39
  208.6 14.7 %collective-permute-start.38 = (f32[3,16,128]{2,1,0:T(8,128)S(1)}, f32[3,16,128]{2,1,0:T(8,128)S(1)}, u32[]{:S(2)}, u32[]{:S(2)}) collective-permute-start(f32[3,16,128]{2,1,0:T(8,128)S(1)} %get-tuple-element.776), channel_id=1, source_target_pairs={{8,0},{16,8},{24,16},{32,24},{40,32},{48,40},{56,48},{64,56},{72,6... | collective-permute-start | bytes 73736 | tf_op jit(solution)/shard_map/ppermute | solution.py:39
  226.3 17.4 %collective-permute-start.42 = (f32[3,2,128]{2,1,0:T(2,128)S(1)}, f32[3,2,128]{2,1,0:T(2,128)S(1)}, u32[]{:S(2)}, u32[]{:S(2)}) collective-permute-start(f32[3,2,128]{2,1,0:T(2,128)S(1)} %bitcast.1232), channel_id=1, source_target_pairs={{1,0},{3,2},{5,4},{7,6},{9,8},{11,10},{13,12},{15,14},{17,16},{19,... | collective-permute-start | bytes 9224 | tf_op jit(solution)/shard_map/ppermute | solution.py:39
  229.1 14.7 %collective-permute-start.44 = (f32[3,16,128]{2,1,0:T(8,128)S(1)}, f32[3,16,128]{2,1,0:T(8,128)S(1)}, u32[]{:S(2)}, u32[]{:S(2)}) collective-permute-start(f32[3,16,128]{2,1,0:T(8,128)S(1)} %get-tuple-element.771), channel_id=1, source_target_pairs={{8,0},{16,8},{24,16},{32,24},{40,32},{48,40},{56,48},{64,56},{72,6... | collective-permute-start | bytes 73736 | tf_op jit(solution)/shard_map/ppermute | solution.py:39
  246.9 17.7 %collective-permute-start.60 = (f32[3,2,128]{2,1,0:T(2,128)S(1)}, f32[3,2,128]{2,1,0:T(2,128)S(1)}, u32[]{:S(2)}, u32[]{:S(2)}) collective-permute-start(f32[3,2,128]{2,1,0:T(2,128)S(1)} %bitcast.1233), channel_id=1, source_target_pairs={{1,0},{3,2},{5,4},{7,6},{9,8},{11,10},{13,12},{15,14},{17,16},{19,... | collective-permute-start | bytes 9224 | tf_op jit(solution)/shard_map/ppermute | solution.py:39
  249.7 15.0 %collective-permute-start.62 = (f32[3,16,128]{2,1,0:T(8,128)S(1)}, f32[3,16,128]{2,1,0:T(8,128)S(1)}, u32[]{:S(2)}, u32[]{:S(2)}) collective-permute-start(f32[3,16,128]{2,1,0:T(8,128)S(1)} %get-tuple-element.766), channel_id=1, source_target_pairs={{8,0},{16,8},{24,16},{32,24},{40,32},{48,40},{56,48},{64,56},{72,6... | collective-permute-start | bytes 73736 | tf_op jit(solution)/shard_map/ppermute | solution.py:39
  267.7 17.7 %collective-permute-start.66 = (f32[3,2,128]{2,1,0:T(2,128)S(1)}, f32[3,2,128]{2,1,0:T(2,128)S(1)}, u32[]{:S(2)}, u32[]{:S(2)}) collective-permute-start(f32[3,2,128]{2,1,0:T(2,128)S(1)} %bitcast.1234), channel_id=1, source_target_pairs={{1,0},{3,2},{5,4},{7,6},{9,8},{11,10},{13,12},{15,14},{17,16},{19,... | collective-permute-start | bytes 9224 | tf_op jit(solution)/shard_map/ppermute | solution.py:39
  270.5 15.0 %collective-permute-start.68 = (f32[3,16,128]{2,1,0:T(8,128)S(1)}, f32[3,16,128]{2,1,0:T(8,128)S(1)}, u32[]{:S(2)}, u32[]{:S(2)}) collective-permute-start(f32[3,16,128]{2,1,0:T(8,128)S(1)} %get-tuple-element.761), channel_id=1, source_target_pairs={{8,0},{16,8},{24,16},{32,24},{40,32},{48,40},{56,48},{64,56},{72,6... | collective-permute-start | bytes 73736 | tf_op jit(solution)/shard_map/ppermute | solution.py:39
  288.6 17.7 %collective-permute-start.84 = (f32[3,2,128]{2,1,0:T(2,128)S(1)}, f32[3,2,128]{2,1,0:T(2,128)S(1)}, u32[]{:S(2)}, u32[]{:S(2)}) collective-permute-start(f32[3,2,128]{2,1,0:T(2,128)S(1)} %bitcast.1235), channel_id=1, source_target_pairs={{1,0},{3,2},{5,4},{7,6},{9,8},{11,10},{13,12},{15,14},{17,16},{19,... | collective-permute-start | bytes 9224 | tf_op jit(solution)/shard_map/ppermute | solution.py:39
  291.4 15.0 %collective-permute-start.86 = (f32[3,16,128]{2,1,0:T(8,128)S(1)}, f32[3,16,128]{2,1,0:T(8,128)S(1)}, u32[]{:S(2)}, u32[]{:S(2)}) collective-permute-start(f32[3,16,128]{2,1,0:T(8,128)S(1)} %get-tuple-element.756), channel_id=1, source_target_pairs={{8,0},{16,8},{24,16},{32,24},{40,32},{48,40},{56,48},{64,56},{72,6... | collective-permute-start | bytes 73736 | tf_op jit(solution)/shard_map/ppermute | solution.py:39
  413.7 15.9 %collective-permute-start.90 = (f32[3,2,128]{2,1,0:T(2,128)S(1)}, f32[3,2,128]{2,1,0:T(2,128)S(1)}, u32[]{:S(2)}, u32[]{:S(2)}) collective-permute-start(f32[3,2,128]{2,1,0:T(2,128)S(1)} %bitcast.1223), channel_id=1, source_target_pairs={{1,0},{3,2},{5,4},{7,6},{9,8},{11,10},{13,12},{15,14},{17,16},{19,... | collective-permute-start | bytes 9224 | tf_op jit(solution)/shard_map/ppermute | solution.py:39
  (69 other events, 614.6 us)
where the time goes:
time: 435 us; the launch traced here: 432 us
  starting transfers between devices  274 us (63%)
  blocking collectives  103 us (24%)
  local copies, waits for them, and re-layouts  18 us (4%)
  other arithmetic  16.7 us (4%)
  waiting for transfers between devices  16.1 us (4%)
    ppermute x48, starting transfers between devices, passed_along(): return lax.ppermute(block, axis, route)  136 us
    psum x2, blocking collectives, by_axis(): return functools.reduce(lax.psum, axes, x)  103 us
    ppermute x24, starting transfers between devices, padded_2(): lax.ppermute(last, axis, up)  102 us
    ppermute x24, starting transfers between devices, padded_2(): lax.ppermute(initial, axis, [(b, a) for a, b in up])  31.4 us
    ppermute x48, waiting for transfers between devices, passed_along(): return lax.ppermute(block, axis, route)  8.81 us
  transfers between devices with their start and end apart: 97, of which 14 were waited for; matrix products, arithmetic and copies ran while one was open for 2% of the time, Pallas kernels for 0%

commit v1 on v0

v1 whole, which is shorter than its diff:
```python
import functools

import jax
import jax.numpy as jnp
from jax import lax
from jax.experimental import pallas as pl
from jax.experimental.pallas import tpu as pltpu
from jax.sharding import Mesh
from jax.sharding import PartitionSpec as P

LANES = 128
HALO = 10
OHALO = 8
PAD = 8
UNSEEN = 1e9
SEEN_BELOW = 1e8
BF, F32 = jnp.bfloat16, jnp.float32

SEGS = (3, 1, 2, 0)
XT = 7
OT = 9
OBS0 = XT * len(SEGS)
REACH = (OBS0 + 2 * OT, OBS0 + OT, 2 * XT)


def lane_ids(shape):
    return lax.broadcasted_iota(jnp.int32, shape, len(shape) - 1)


def split_bf16(x):
    high = x.astype(BF)
    return high, (x - high.astype(F32)).astype(BF)


def pack(strips, width):
    out = jnp.zeros(strips[0].shape, F32)
    lane = lane_ids(out.shape)
    for j, strip in enumerate(strips):
        start = 2 * width * j
        moved = pltpu.roll(strip, (start + width) % LANES, 1)
        out = jnp.where((lane >= start) & (lane < start + 2 * width), moved, out)
    return out


def unpack(tile, j, width):
    back = pltpu.roll(tile, (-(2 * width * j + width)) % LANES, 1)
    lane = lane_ids(back.shape)
    return jnp.where((lane < width) | (lane >= LANES - width), back, 0.0)


def outgoing(cols, ckpt, obs, mask, drag, send, coded):
    segs, rows, levels = obs.shape[0], obs.shape[1], obs.shape[2]
    lane = lane_ids((levels, LANES))
    low = lane < LANES // 2
    observed = []
    for s in range(segs):
        for r in range(rows):
            value = jnp.where(mask[s, r] > 0, obs[s, r], UNSEEN)
            coded[s * rows + r] = value
            observed.append(value)
    coded[segs * rows] = jnp.broadcast_to(drag[...], (levels, LANES))
    obs_tiles = []
    for pair in (SEGS[:2], SEGS[2:]):
        strips = []
        for s in pair:
            for r in range(rows):
                strips.extend(part.astype(F32) for part in split_bf16(observed[s * rows + r]))
        obs_tiles.append(pack(strips, OHALO).astype(BF))
    zero = jnp.zeros((levels, LANES), F32)
    for c in range(cols):
        strips = []
        for comp in range(3):
            for r in range(rows):
                own = ckpt[comp, r, :, c * LANES : (c + 1) * LANES]
                for z in range(2):
                    send[c, z, comp * rows + r] = own
                left = ckpt[comp, r, :, (c - 1) * LANES : c * LANES].astype(F32) if c else zero
                right = (
                    ckpt[comp, r, :, (c + 1) * LANES : (c + 2) * LANES].astype(F32)
                    if c < cols - 1
                    else zero
                )
                strips.append(jnp.where(low, right, left))
        tiles = [pack(strips, HALO).astype(BF)] + obs_tiles
        for t, tile in enumerate(tiles):
            for z in range(2):
                send[c, z, 6 + t] = tile


def arrange(cols, place, got, coded, theirs, one, two, three):
    col, core = place[1], place[2]
    levels, rows = coded.shape[1], 2
    outs = (one, two, three)

    def put(t, g, tile):
        for out in outs:
            if t < out.shape[0]:
                out[t, g * levels : (g + 1) * levels] = tile

    lane = lane_ids((levels, LANES))
    left = (lane % (2 * OHALO)) < OHALO
    west = jnp.maximum(col - 1, 0)
    east = jnp.minimum(col + 1, cols - 1)
    for g in range(2):
        for k, s in enumerate(SEGS):
            for t in range(XT):
                put(k * XT + t, g, got[s * 2 + g, t])
        mine = core == g
        for k in range(2):
            base = OBS0 + k * OT
            for n, s in enumerate(SEGS[2 * k : 2 * k + 2]):
                for r in range(rows):
                    value = jnp.where(mine, coded[s * rows + r], theirs[s * rows + r])
                    for e, part in enumerate(split_bf16(value)):
                        put(base + (n * rows + r) * 2 + e, g, part)
            strip = jnp.where(
                left, got[west * 2 + g, 7 + k].astype(F32), got[east * 2 + g, 7 + k].astype(F32)
            )
            put(base + OT - 1, g, strip.astype(BF))


def chunk(pair, first, dims, place, coded, theirs, one, r1, r2, r3, swapped, *rest):
    if first:
        lam_out, sums_out, x0, x1, la, lb, obs, decay = rest
    else:
        lam_own, l1, l2, lswap, sums_in, grad, message, x0, x1, la, lb, obs, decay = rest
    total_rows, total_cols = dims
    gx, col, core = place[0], place[1], place[2]
    levels = one.shape[1]
    half = levels // 2
    wide = 2 * LANES
    got = (r1, r2, r3)
    starts = (0, REACH[0], REACH[0] + REACH[1])

    for buf in (x0, x1, la, lb):
        edge = jnp.zeros(buf.shape[:2] + (PAD, wide), F32)
        buf[:, :, :PAD] = edge
        buf[:, :, PAD + levels :] = edge
    for g in range(2):
        k = jnp.where(core == g, coded[coded.shape[0] - 1], theirs[theirs.shape[0] - 1])
        both = jnp.concatenate([k, k], axis=1)
        decay[g * half : (g + 1) * half] = 0.4 - 0.1 * both

    lane = lane_ids((1, wide))
    column = jnp.where(lane < LANES, lane, jnp.where(lane < LANES + HALO, lane, lane - wide))
    held = (lane < LANES + HALO) | (lane >= wide - HALO)
    column = column + col * LANES
    inside = jnp.where(held & (column >= 0) & (column < total_cols), 1.0, 0.0).astype(F32)
    across = inside * (1.0 + 2.0 * column.astype(F32) / total_cols)

    def row_of(i, reach):
        row = gx * 2 + i - reach
        exists = jnp.where((row >= 0) & (row < total_rows), 1.0, 0.0).astype(F32)
        return row.astype(F32), exists

    def tile(b, t, arrays, swap, offsets):
        if b == 0:
            return arrays[0][t].astype(F32)
        mine = arrays[abs(b)][t].astype(F32)
        other = swap[offsets[abs(b) - 1] + t].astype(F32)
        return jnp.where(core == (0 if b < 0 else 1), mine, other)

    def state_tile(b, t):
        return tile(b, t, (one,) + got, swapped, starts)

    def load_state(seg, reach):
        base = SEGS.index(seg) * XT
        blocks = reach // 2
        for b in range(-blocks, blocks + 1):
            strip = state_tile(b, base + 6)
            for comp in range(3):
                for r in range(2):
                    j = comp * 2 + r
                    row = 2 * (b + blocks) + r
                    x0[comp, row, PAD : PAD + levels, :LANES] = state_tile(b, base + j)
                    x0[comp, row, PAD : PAD + levels, LANES:] = unpack(strip, j, HALO)

    def load_obs(seg, reach):
        n = SEGS.index(seg)
        base = OBS0 + (n // 2) * OT
        blocks = reach // 2
        for b in range(-blocks, blocks + 1):
            strip = state_tile(b, base + OT - 1)
            for r in range(2):
                row = 2 * (b + blocks) + r
                j = ((n % 2) * 2 + r) * 2
                obs[row, :, :LANES] = state_tile(b, base + j) + state_tile(b, base + j + 1)
                obs[row, :, LANES:] = unpack(strip, j, OHALO) + unpack(strip, j + 1, OHALO)

    def east(a):
        return pltpu.roll(a, wide - 1, 1)

    def west(a):
        return pltpu.roll(a, 1, 1)

    def here(buf, comp, i, j):
        return buf[comp, i, PAD + 8 * j : PAD + 8 * j + 8]

    def mixed(buf, comp, i, j):
        lo = PAD + 8 * j
        return buf[comp, i, lo + 1 : lo + 9] + buf[comp, i, lo - 1 : lo + 7]

    def step_h(x, i, j):
        h, u, v = here(x, 0, i, j), here(x, 1, i, j), here(x, 2, i, j)
        he, hw, ue, uw = east(h), west(h), east(u), west(u)
        hn, hs = here(x, 0, i + 1, j), here(x, 0, i - 1, j)
        vn, vs = here(x, 2, i + 1, j), here(x, 2, i - 1, j)
        new = (
            0.4 * h
            + 0.05
            * ((hn + hs) + (he + hw) - (ue - uw) - (vn - vs) - (he * ue - hw * uw) - (hn * vn - hs * vs))
            + 0.2 * mixed(x, 0, i, j)
        )
        return new, (h, u, v, he, hw, ue, uw, hn, hs, vn, vs)

    def forward(reach):
        def body(i, carry):
            row, exists = row_of(i, reach - 1)
            mask = inside * exists
            spin = 0.1 * (0.2 + 0.1 * row / total_rows)
            for j in range(levels // 8):
                h_new, (h, u, v, he, hw, ue, uw, hn, hs, vn, vs) = step_h(x0, i + 1, j)
                un, us = here(x0, 1, i + 2, j), here(x0, 1, i, j)
                ve, vw = east(v), west(v)
                keep = decay[8 * j : 8 * j + 8]
                u_new = (
                    keep * u
                    + 0.05 * ((un + us) + (ue + uw) - (he - hw) - u * (ue - uw) - v * (un - us))
                    + spin * v
                    + 0.2 * mixed(x0, 1, i + 1, j)
                )
                v_new = (
                    keep * v
                    + 0.05 * ((vn + vs) + (ve + vw) - (hn - hs) - u * (ve - vw) - v * (vn - vs))
                    - spin * u
                    + 0.2 * mixed(x0, 2, i + 1, j)
                )
                lo = PAD + 8 * j
                x1[0, i, lo : lo + 8] = h_new * mask
                x1[1, i, lo : lo + 8] = u_new * mask
                x1[2, i, lo : lo + 8] = v_new * mask
            return carry

        lax.fori_loop(0, 2 * reach, body, 0)

    def force(reach, add, cost):
        def body(i, carry):
            row, exists = row_of(i, reach)
            scale = across * (exists * (1.0 + 2.0 * row / total_rows))
            own = jnp.where((i >= reach) & (i < reach + 2), 0.5, 0.0).astype(F32)
            new = []
            for j in range(levels // 8):
                h2, _ = step_h(x1, i + 1, j)
                seen = obs[i, 8 * j : 8 * j + 8]
                miss = jnp.where(seen < SEEN_BELOW, h2 - seen, 0.0)
                g = scale * miss
                lo = PAD + 8 * j
                if add:
                    la[0, i, lo : lo + 8] = la[0, i, lo : lo + 8] + g
                else:
                    la[0, i, lo : lo + 8] = g
                    la[1, i, lo : lo + 8] = jnp.zeros_like(g)
                    la[2, i, lo : lo + 8] = jnp.zeros_like(g)
                new.append(carry[j] + own * (g * miss)[:, :LANES])
            return tuple(new)

        return lax.fori_loop(0, 2 * reach + 2, body, cost)

    def backward(lam, x, shift, out, count, reach):
        def body(i, carry):
            row, exists = row_of(i, reach)
            mask = inside * exists
            spin = 0.1 * (0.2 + 0.1 * row / total_rows)
            p = i + shift
            for j in range(levels // 8):
                a, b, c = (here(lam, comp, i + 1, j) for comp in range(3))
                h, u, v = (here(x, comp, p, j) for comp in range(3))
                ae, aw, an, as_ = east(a), west(a), here(lam, 0, i + 2, j), here(lam, 0, i, j)
                be, bw, bn, bs = east(b), west(b), here(lam, 1, i + 2, j), here(lam, 1, i, j)
                ce, cw, cn, cs = east(c), west(c), here(lam, 2, i + 2, j), here(lam, 2, i, j)
                ue, uw, un, us = east(u), west(u), here(x, 1, p + 1, j), here(x, 1, p - 1, j)
                ve, vw, vn, vs = east(v), west(v), here(x, 2, p + 1, j), here(x, 2, p - 1, j)
                keep = decay[8 * j : 8 * j + 8]
                ax, ay = ae - aw, an - as_
                deep = 1.0 + h
                a_new = (
                    0.4 * a
                    + 0.05 * ((an + as_) + (ae + aw) + (be - bw) + (cn - cs) + u * ax + v * ay)
                    + 0.2 * mixed(lam, 0, i + 1, j)
                )
                b_new = (
                    keep * b
                    + 0.05
                    * (
                        (bn + bs)
                        + (be + bw)
                        - b * (ue - uw)
                        + (ue * be - uw * bw)
                        + (vn * bn - vs * bs)
                        - c * (ve - vw)
                        + deep * ax
                    )
                    - spin * c
                    + 0.2 * mixed(lam, 1, i + 1, j)
                )
                c_new = (
                    keep * c
                    + 0.05
                    * (
                        (cn + cs)
                        + (ce + cw)
                        - b * (un - us)
                        + (ue * ce - uw * cw)
                        - c * (vn - vs)
                        + (vn * cn - vs * cs)
                        + deep * ay
                    )
                    + spin * b
                    + 0.2 * mixed(lam, 2, i + 1, j)
                )
                lo = PAD + 8 * j
                out[0, i, lo : lo + 8] = a_new * mask
                out[1, i, lo : lo + 8] = b_new * mask
                out[2, i, lo : lo + 8] = c_new * mask
            return carry

        lax.fori_loop(0, count, body, 0)

    def drag_terms(lam, lrow, x, xrow, total):
        new = []
        for j in range(levels // 8):
            t = total[j]
            for r in range(2):
                for comp in (1, 2):
                    mine = here(lam, comp, lrow + r, j)[:, :LANES]
                    t = t + mine * here(x, comp, xrow + r, j)[:, :LANES]
            new.append(t)
        return new

    zero = tuple(jnp.zeros((8, LANES), F32) for _ in range(levels // 8))
    cost, pulled = zero, list(zero)
    if not first:
        lams = (lam_own, l1, l2)
        for b in range(-2, 3):
            strip = tile(b, 6, lams, lswap, (0, XT))
            for comp in range(3):
                for r in range(2):
                    j = comp * 2 + r
                    row = 2 * (b + 2) + r
                    main = tile(b, j, lams, lswap, (0, XT))
                    la[comp, row, PAD : PAD + levels, :LANES] = main
                    la[comp, row, PAD : PAD + levels, LANES:] = unpack(strip, j, HALO)

    far, near = pair
    load_state(far, 6)
    load_obs(far, 4)
    forward(6)
    cost = force(4, not first, cost)
    pulled = drag_terms(la, 4, x1, 5, pulled)
    backward(la, x1, 2, lb, 8, 3)
    pulled = drag_terms(lb, 3, x0, 6, pulled)
    backward(lb, x0, 4, la, 6, 2)
    load_state(near, 4)
    load_obs(near, 2)
    forward(4)
    cost = force(2, True, cost)
    pulled = drag_terms(la, 2, x1, 3, pulled)
    backward(la, x1, 2, lb, 4, 1)
    pulled = drag_terms(lb, 1, x0, 4, pulled)
    backward(lb, x0, 4, la, 2, 0)

    if first:
        strips = []
        for comp in range(3):
            for r in range(2):
                lam_out[comp * 2 + r] = la[comp, r, PAD : PAD + levels, :LANES]
                strips.append(la[comp, r, PAD : PAD + levels, LANES:])
        lam_out[6] = pack(strips, HALO)
        for j in range(levels // 8):
            sums_out[0, 8 * j : 8 * j + 8] = cost[j]
            sums_out[1, 8 * j : 8 * j + 8] = pulled[j]
    else:
        start = pl.multiple_of(core * half, half)
        for comp in range(3):
            for r in range(2):
                grad[comp, r] = la[comp, r, pl.ds(PAD + start, half), :LANES]
        for j in range(levels // 8):
            obs[0, 8 * j : 8 * j + 8, :LANES] = cost[j] + sums_in[0, 8 * j : 8 * j + 8]
            obs[1, 8 * j : 8 * j + 8, :LANES] = pulled[j] + sums_in[1, 8 * j : 8 * j + 8]
        area = 1.0 / (total_rows * total_cols)
        line = jnp.zeros((1, LANES), F32)
        for k, factor in ((0, area), (1, -0.1 * area)):
            part = jnp.sum(obs[k, pl.ds(start, half), :LANES], axis=1, keepdims=True) * factor
            level = lax.broadcasted_iota(jnp.int32, (half, LANES), 0) + k * half
            line = line + jnp.sum(
                jnp.where(level == lane_ids((half, LANES)), part, 0.0), axis=0, keepdims=True
            )
        for n in range(message.shape[0]):
            message[n] = jnp.broadcast_to(line, message.shape[1:])


def vmem():
    return pl.BlockSpec(memory_space=pltpu.VMEM)


def smem():
    return pl.BlockSpec(memory_space=pltpu.SMEM)


def call(kernel, outs, places, vmems, scratch=(), limit=None):
    return pl.pallas_call(
        kernel,
        out_shape=outs,
        in_specs=[smem()] * len(places) + [vmem()] * len(vmems),
        out_specs=jax.tree.map(lambda _: vmem(), outs),
        scratch_shapes=list(scratch),
        compiler_params=pltpu.CompilerParams(vmem_limit_bytes=limit),
    )(*places, *vmems)


def on_device(checkpoints, obs_values, obs_mask, drag):
    segs, levels, rows, lanes = obs_values.shape
    cols, cores = lax.axis_size("col"), lax.axis_size("gz")
    outer, inner = lax.axis_size("gxo"), lax.axis_size("gxi")
    lat = outer * inner
    dims = (rows * lat, lanes * cols)
    place = jnp.stack(
        [lax.axis_index("gxo") * inner + lax.axis_index("gxi"), lax.axis_index("col"), lax.axis_index("gz")]
    ).astype(jnp.int32)

    def sds(shape, dtype=F32):
        return jax.ShapeDtypeStruct(shape, dtype)

    def toward(block, distance):
        route = []
        for i in range(lat):
            for core, step in ((0, distance), (1, -distance)):
                if 0 <= i + step < lat:
                    route.append((i * cores + core, (i + step) * cores + core))
        return lax.ppermute(block, ("gxo", "gxi", "gz"), route)

    def swap(block):
        return lax.ppermute(block, "gz", [(0, 1), (1, 0)])

    send, coded = call(
        functools.partial(outgoing, cols),
        (sds((cols, cores, 9, levels, LANES), BF), sds((segs * rows + 1, levels, LANES))),
        (),
        (
            checkpoints[0].transpose(0, 2, 1, 3),
            obs_values.transpose(0, 2, 1, 3),
            obs_mask.transpose(0, 2, 1, 3),
            drag[:, None],
        ),
    )
    theirs = swap(coded)
    got = lax.all_to_all(
        send.reshape(cols * cores, 9, levels, LANES), ("col", "gz"), 0, 0, tiled=True
    )
    full = levels * cores
    ones = call(
        functools.partial(arrange, cols),
        tuple(sds((n, full, LANES), BF) for n in REACH),
        (place,),
        (got, coded, theirs),
    )
    came = [toward(block, d + 1) for d, block in enumerate(ones)]
    swapped = swap(jnp.concatenate(came))

    def scratch():
        return [
            pltpu.VMEM((3, 14, full + 2 * PAD, 2 * LANES), F32),
            pltpu.VMEM((3, 12, full + 2 * PAD, 2 * LANES), F32),
            pltpu.VMEM((3, 10, full + 2 * PAD, 2 * LANES), F32),
            pltpu.VMEM((3, 8, full + 2 * PAD, 2 * LANES), F32),
            pltpu.VMEM((10, full, 2 * LANES), F32),
            pltpu.VMEM((full, 2 * LANES), F32),
        ]

    data = (coded, theirs, ones[0], *came, swapped)
    lam, sums = call(
        functools.partial(chunk, (3, 2), True, dims),
        (sds((XT, full, LANES)), sds((2, full, LANES))),
        (place,),
        data,
        scratch(),
    )
    near, next_ = toward(lam, 1), toward(lam, 2)
    lswap = swap(jnp.concatenate([near, next_]))
    team = inner * cols
    grad, message = call(
        functools.partial(chunk, (1, 0), False, dims),
        (sds((3, rows, levels, LANES)), sds((team, 8, LANES))),
        (place,),
        data + (lam, near, next_, lswap, sums),
        scratch(),
    )
    near_sum = jnp.sum(lax.all_to_all(message, ("gxi", "col"), 0, 0, tiled=True), axis=0)
    spread = jnp.broadcast_to(near_sum, (outer,) + near_sum.shape)
    total = jnp.sum(lax.all_to_all(spread, "gxo", 0, 0, tiled=True), axis=0)[0]
    return grad.transpose(0, 2, 1, 3), total[:levels], total[levels : 2 * levels]


def solution(mesh):
    inner = 4
    sizes = dict(mesh.shape)
    fine = Mesh(
        mesh.devices.reshape(sizes["ens"], sizes["gx"] // inner, inner, sizes["col"], sizes["gz"]),
        ("ens", "gxo", "gxi", "col", "gz"),
    )
    lat = ("gxo", "gxi")
    return jax.shard_map(
        on_device,
        mesh=fine,
        in_specs=(
            P(("ens", "col"), None, "gz", lat, None),
            P("ens", "gz", lat, "col"),
            P("ens", "gz", lat, "col"),
            P(("ens", "gz")),
        ),
        out_specs=(P("ens", "gz", lat, "col"), P(("ens", "gz")), P(("ens", "gz"))),
        check_vma=False,
    )
```

time: 435 us -> 170 us (0.39)
  starting transfers between devices: 274 us -> 78.2 us
  blocking collectives: 103 us -> 18.8 us
  Pallas kernels: 0 us -> 25.7 us
  waiting for transfers between devices: 16.1 us -> 35.6 us
  other arithmetic: 16.7 us -> 0.8 us
  local copies, waits for them, and re-layouts: 18 us -> 9.65 us
    ppermute x96 -> x8, starting transfers between devices: 270 us -> 41.1 us  [the longest x5 34.8 us: toward(): return lax.ppermute(block, ('gxo', 'gxi', 'gz'), route)]
    psum x2 -> x0, blocking collectives: 103 us -> none  [by_axis(): return functools.reduce(lax.psum, axes, x)]
    all_to_all x1 -> x2, starting transfers between devices: 4.71 us -> 37.1 us  [the longest x1 32.4 us: on_device(): total = jnp.sum(lax.all_to_all(spread, 'gxo', 0, 0, tiled=True), axis=0)[0]]
    pallas_call x0 -> x4, Pallas kernels: none -> 25.7 us  [call(): pl.pallas_call(kernel, out_shape=outs, in_specs=[smem()] * len(places) +...]
    all_to_all x1 -> x2, waiting for transfers between devices: 4.02 us -> 26.4 us  [the longest x1 21.9 us: on_device(): total = jnp.sum(lax.all_to_all(spread, 'gxo', 0, 0, tiled=True), axis=0)[0]]
    all_to_all x0 -> x1, blocking collectives: none -> 18.8 us  [on_device(): lax.all_to_all(message, ('gxi', 'col'), 0, 0, tiled=True)]
    scatter-add x35 -> x0, local copies, waits for them, and re-layouts: 5.8 us -> none  [the longest x18 5.02 us: halo_back(): return inner.at[:, :, :, -1].add(west).at[:, :, :, 0].add(east)]
    ppermute x96 -> x8, waiting for transfers between devices: 12.1 us -> 9.25 us  [the longest x5 5.31 us: toward(): return lax.ppermute(block, ('gxo', 'gxi', 'gz'), route)]
  transfers between devices with their start and end apart: 97 -> 10, of which waited for: 14 -> 7; matrix products, arithmetic and copies ran while one was open for 2% -> 1% of each run, Pallas kernels for 0% -> 0%
where the time goes in v1:
time: 170 us
  starting transfers between devices  78.2 us (46%)
  waiting for transfers between devices  35.6 us (21%)
  Pallas kernels  25.7 us (15%)
  blocking collectives  18.8 us (11%)
  local copies, waits for them, and re-layouts  9.65 us (6%)
    ppermute x5, starting transfers between devices, toward(): return lax.ppermute(block, ('gxo', 'gxi', 'gz'), route)  34.8 us
    all_to_all x1, starting transfers between devices, on_device(): total = jnp.sum(lax.all_to_all(spread, 'gxo', 0, 0, tiled=True), axis=0)[0]  32.4 us
    pallas_call x4, Pallas kernels, call(): pl.pallas_call(kernel, out_shape=outs, in_specs=[smem()] * len(places) +...  25.7 us
    all_to_all x1, waiting for transfers between devices, on_device(): total = jnp.sum(lax.all_to_all(spread, 'gxo', 0, 0, tiled=True), axis=0)[0]  21.9 us
    all_to_all x1, blocking collectives, on_device(): lax.all_to_all(message, ('gxi', 'col'), 0, 0, tiled=True)  18.8 us
    unnamed x32, local copies, waits for them, and re-layouts  7.78 us
    ppermute x3, starting transfers between devices, swap(): return lax.ppermute(block, 'gz', [(0, 1), (1, 0)])  6.31 us
    ppermute x5, waiting for transfers between devices, toward(): return lax.ppermute(block, ('gxo', 'gxi', 'gz'), route)  5.31 us
  transfers between devices with their start and end apart: 10, of which 7 were waited for; matrix products, arithmetic and copies ran while one was open for 1% of the time, Pallas kernels for 0%

profile of v1, /device:TPU:40, one launch (start us, length us, event | category | flops | bytes accessed | tf_op | source)
XLA Modules:
  0.0 169.6 jit_solution(5849145213386223915)
XLA Ops:
  0.6 0.6 copy-done.13
  1.3 0.7 copy.15.drag
  2.0 1.5 copy.22
  3.5 0.6 copy.21
  4.1 0.6 copy.20
  4.7 1.8 %shard_map.67 = (bf16[4,2,9,16,128]{4,3,2,1,0:T(8,128)(2,1)}, f32[9,16,128]{2,1,0:T(8,128)}) custom-call(bf16[3,2,16,512]{3,2,1,0:T(8,128)(2,1)} %bitcast.21, f32[4,2,16,128]{3,2,1,0:T(8,128)} %bitcast.23, s32[4,2,16,128]{3,2,1,0:T(8,128)} %bitcast.24, f32[16,1]{1,0:T(8,128)} %copy.15.drag), custom_call_target="tpu_custom_call" | custom-call | tf_op jit(solution)/shard_map/pallas_call | solution.py:411
  6.5 4.7 %all-to-all-start = ((bf16[8,9,16,128]{3,2,1,0:T(8,128)(2,1)}), bf16[8,9,16,128]{3,2,1,0:T(8,128)(2,1)S(1)}, u32[]{:S(2)}, u32[]{:S(2)}) async-start(bf16[8,9,16,128]{3,2,1,0:T(8,128)(2,1)} %bitcast.22), calls=%async_computation | async-start | bytes 589824 | tf_op jit(solution)/shard_map/all_to_all | solution.py:457
  11.2 2.4 %collective-permute-start = (f32[9,16,128]{2,1,0:T(8,128)S(1)}, f32[9,16,128]{2,1,0:T(8,128)S(1)}, u32[]{:S(2)}, u32[]{:S(2)}) collective-permute-start(f32[9,16,128]{2,1,0:T(8,128)S(1)} %copy-done.5), channel_id=1, source_target_pairs={{0,1},{1,0},{2,3},{3,2},{4,5},{5,4},{6,7},{7,6},{8,9},{9,8},{10,11... | collective-permute-start | bytes 221192 | tf_op jit(solution)/shard_map/ppermute | solution.py:443
  13.7 0.7 pad_add_fusion.place
  14.6 4.5 %all-to-all-done.got = bf16[8,9,16,128]{3,2,1,0:T(8,128)(2,1)S(1)} async-done(((bf16[8,9,16,128]{3,2,1,0:T(8,128)(2,1)}), bf16[8,9,16,128]{3,2,1,0:T(8,128)(2,1)S(1)}, u32[]{:S(2)}, u32[]{:S(2)}) %all-to-all-start) | async-done | bytes 294944 | tf_op jit(solution)/shard_map/all_to_all | solution.py:457
  19.1 0.7 copy-done.3
  19.8 2.0 %shard_map.68 = (bf16[46,32,128]{2,1,0:T(8,128)(2,1)}, bf16[37,32,128]{2,1,0:T(8,128)(2,1)}, bf16[14,32,128]{2,1,0:T(8,128)(2,1)}) custom-call(s32[3]{0:T(128)} %pad_add_fusion.place, bf16[8,9,16,128]{3,2,1,0:T(8,128)(2,1)} %copy-done.3, f32[9,16,128]{2,1,0:T(8,128)} %get-tuple-element.12.coded, f32[9,16,128]{2,1,0:T(8,128)} %copy-done.6), custom_call_target="tpu_custom_call" | custom-call | tf_op jit(solution)/shard_map/pallas_call | solution.py:411
  21.8 4.7 %collective-permute-start.1 = (bf16[46,32,128]{2,1,0:T(8,128)(2,1)}, bf16[46,32,128]{2,1,0:T(8,128)(2,1)S(1)}, u32[]{:S(2)}, u32[]{:S(2)}) collective-permute-start(bf16[46,32,128]{2,1,0:T(8,128)(2,1)} %get-tuple-element.14.one), channel_id=1, source_target_pairs={{0,8},{8,16},{9,1},{16,24},{17,9},{24,32},{25,17},{32,40},{33,25},... | collective-permute-start | bytes 1130504 | tf_op jit(solution)/shard_map/ppermute | solution.py:440
  26.5 6.9 %collective-permute-start.2 = (bf16[37,32,128]{2,1,0:T(8,128)(2,1)}, bf16[37,32,128]{2,1,0:T(8,128)(2,1)S(1)}, u32[]{:S(2)}, u32[]{:S(2)}) collective-permute-start(bf16[37,32,128]{2,1,0:T(8,128)(2,1)} %get-tuple-element.15), channel_id=1, source_target_pairs={{0,16},{8,24},{16,32},{17,1},{24,40},{25,9},{32,48},{33,17},{40,56... | collective-permute-start | bytes 909320 | tf_op jit(solution)/shard_map/ppermute | solution.py:440
  33.5 10.3 %collective-permute-start.3 = (bf16[14,32,128]{2,1,0:T(8,128)(2,1)}, bf16[14,32,128]{2,1,0:T(8,128)(2,1)S(1)}, u32[]{:S(2)}, u32[]{:S(2)}) collective-permute-start(bf16[14,32,128]{2,1,0:T(8,128)(2,1)} %get-tuple-element.16), channel_id=1, source_target_pairs={{0,24},{8,32},{16,40},{24,48},{25,1},{32,56},{33,9},{40,64},{41,17... | collective-permute-start | bytes 344072 | tf_op jit(solution)/shard_map/ppermute | solution.py:440
  43.8 2.7 %collective-permute-done.3.r3 = bf16[14,32,128]{2,1,0:T(8,128)(2,1)S(1)} collective-permute-done((bf16[14,32,128]{2,1,0:T(8,128)(2,1)}, bf16[14,32,128]{2,1,0:T(8,128)(2,1)S(1)}, u32[]{:S(2)}, u32[]{:S(2)}) %collective-permute-start.3) | collective-permute-done | bytes 114720 | tf_op jit(solution)/shard_map/ppermute | solution.py:440
  47.4 1.9 %collective-permute-start.4 = (bf16[97,32,128]{2,1,0:T(8,128)(2,1)S(1)}, bf16[97,32,128]{2,1,0:T(8,128)(2,1)S(1)}, u32[]{:S(2)}, u32[]{:S(2)}) collective-permute-start(bf16[97,32,128]{2,1,0:T(8,128)(2,1)S(1)} %pad_maximum_fusion), channel_id=1, source_target_pairs={{0,1},{1,0},{2,3},{3,2},{4,5},{5,4},{6,7},{7,6},{8,9},{9,8},{10,11... | collective-permute-start | bytes 2383880 | tf_op jit(solution)/shard_map/ppermute | solution.py:443
  49.3 2.3 %collective-permute-done.4.swapped = bf16[97,32,128]{2,1,0:T(8,128)(2,1)S(1)} collective-permute-done((bf16[97,32,128]{2,1,0:T(8,128)(2,1)S(1)}, bf16[97,32,128]{2,1,0:T(8,128)(2,1)S(1)}, u32[]{:S(2)}, u32[]{:S(2)}) %collective-permute-start.4) | collective-permute-done | bytes 794656 | tf_op jit(solution)/shard_map/ppermute | solution.py:443
  51.6 0.9 copy-done.1
  52.5 10.8 %shard_map.69 = (f32[7,32,128]{2,1,0:T(8,128)}, f32[2,32,128]{2,1,0:T(8,128)}) custom-call(s32[3]{0:T(128)} %pad_add_fusion.place, f32[9,16,128]{2,1,0:T(8,128)} %get-tuple-element.12.coded, f32[9,16,128]{2,1,0:T(8,128)} %copy-done.6, bf16[46,32,128]{2,1,0:T(8,128)(2,1)} %get-tuple-element.14.one, bf16[46,32,128]{2,1,0:T(8,128)(2,1)} %copy-done, ...), custom_call_target="tpu_custom_call" | custom-call | tf_op jit(solution)/shard_map/pallas_call | solution.py:411
  63.3 8.1 %collective-permute-start.6 = (f32[7,32,128]{2,1,0:T(8,128)}, f32[7,32,128]{2,1,0:T(8,128)S(1)}, u32[]{:S(2)}, u32[]{:S(2)}) collective-permute-start(f32[7,32,128]{2,1,0:T(8,128)} %get-tuple-element.17.rest_0_), channel_id=1, source_target_pairs={{0,16},{8,24},{16,32},{17,1},{24,40},{25,9},{32,48},{33,17},{40,56... | collective-permute-start | bytes 344072 | tf_op jit(solution)/shard_map/ppermute | solution.py:440
  71.4 4.7 %collective-permute-start.5 = (f32[7,32,128]{2,1,0:T(8,128)}, f32[7,32,128]{2,1,0:T(8,128)S(1)}, u32[]{:S(2)}, u32[]{:S(2)}) collective-permute-start(f32[7,32,128]{2,1,0:T(8,128)} %get-tuple-element.17.rest_0_), channel_id=1, source_target_pairs={{0,8},{8,16},{9,1},{16,24},{17,9},{24,32},{25,17},{32,40},{33,25},... | collective-permute-start | bytes 344072 | tf_op jit(solution)/shard_map/ppermute | solution.py:440
  76.2 2.6 %collective-permute-done.5.rest_1_ = f32[7,32,128]{2,1,0:T(8,128)S(1)} collective-permute-done((f32[7,32,128]{2,1,0:T(8,128)}, f32[7,32,128]{2,1,0:T(8,128)S(1)}, u32[]{:S(2)}, u32[]{:S(2)}) %collective-permute-start.5) | collective-permute-done | bytes 114720 | tf_op jit(solution)/shard_map/ppermute | solution.py:440
  78.9 0.6 copy-done.8
  79.5 1.9 %collective-permute-start.7 = (f32[14,32,128]{2,1,0:T(8,128)S(1)}, f32[14,32,128]{2,1,0:T(8,128)S(1)}, u32[]{:S(2)}, u32[]{:S(2)}) collective-permute-start(f32[14,32,128]{2,1,0:T(8,128)S(1)} %pad_maximum_fusion.1), channel_id=1, source_target_pairs={{0,1},{1,0},{2,3},{3,2},{4,5},{5,4},{6,7},{7,6},{8,9},{9,8},{10,11... | collective-permute-start | bytes 688136 | tf_op jit(solution)/shard_map/ppermute | solution.py:443
  81.4 1.5 collective-permute-done.7.rest_3_
  82.9 0.7 copy-done.9
  83.6 11.1 %shard_map.70 = (f32[3,2,16,128]{3,2,1,0:T(8,128)}, f32[16,8,128]{2,1,0:T(8,128)}) custom-call(s32[3]{0:T(128)} %pad_add_fusion.place, f32[9,16,128]{2,1,0:T(8,128)} %get-tuple-element.12.coded, f32[9,16,128]{2,1,0:T(8,128)} %copy-done.6, bf16[46,32,128]{2,1,0:T(8,128)(2,1)} %get-tuple-element.14.one, bf16[46,32,128]{2,1,0:T(8,128)(2,1)} %copy-done, ...), custom_call_target="tpu_custom_call" | custom-call | tf_op jit(solution)/shard_map/pallas_call | solution.py:411
  94.7 18.8 %all_to_all.15 = f32[16,8,128]{2,1,0:T(8,128)S(1)} all-to-all(f32[16,8,128]{2,1,0:T(8,128)} %get-tuple-element.20), channel_id=1, replica_groups=mesh['ens'=2,'gxo'=8,'gxi'=4,'col'=4,'gz'=2] {'gxi','col'}, dimensions={0} | all-to-all | bytes 131072 | tf_op jit(solution)/shard_map/all_to_all | solution.py:498
  114.1 32.4 %all-to-all-start.2 = ((f32[8,8,128]{2,1,0:T(8,128)}), f32[8,8,128]{2,1,0:T(8,128)S(1)}, u32[]{:S(2)}, u32[]{:S(2)}) async-start(f32[8,8,128]{2,1,0:T(8,128)} %broadcast_in_dim.7), calls=%async_computation.2 | async-start | bytes 65536 | tf_op jit(solution)/shard_map/all_to_all | solution.py:500
  146.5 0.6 copy.16
  147.1 21.9 %all-to-all-done.2 = f32[8,8,128]{2,1,0:T(8,128)S(1)} async-done(((f32[8,8,128]{2,1,0:T(8,128)}), f32[8,8,128]{2,1,0:T(8,128)S(1)}, u32[]{:S(2)}, u32[]{:S(2)}) %all-to-all-start.2) | async-done | bytes 32800 | tf_op jit(solution)/shard_map/all_to_all | solution.py:500
  (33 shorter events, 2.4 us)
Async XLA Ops:
  0.6 0.7 copy-start.13
  1.3 2.2 %copy-start.11 = (s32[4,16,2,128]{3,2,1,0:T(2,128)S(1)}, s32[4,16,2,128]{3,2,1,0:T(2,128)}, u32[]{:S(2)}) copy-start(s32[4,16,2,128]{3,2,1,0:T(2,128)} %param.6) | copy-start | bytes 196612
  2.0 2.1 %copy-start.10 = (bf16[1,3,16,2,512]{4,3,2,1,0:T(2,128)(2,1)S(1)}, bf16[1,3,16,2,512]{4,3,2,1,0:T(2,128)(2,1)}, u32[]{:S(2)}) copy-start(bf16[1,3,16,2,512]{4,3,2,1,0:T(2,128)(2,1)} %param.4) | copy-start | bytes 294916
  6.5 4.7 %copy-start.5 = (f32[9,16,128]{2,1,0:T(8,128)S(1)}, f32[9,16,128]{2,1,0:T(8,128)}, u32[]{:S(2)}) copy-start(f32[9,16,128]{2,1,0:T(8,128)} %get-tuple-element.12.coded) | copy-start | bytes 221188
  6.5 12.6 %all-to-all-start = ((bf16[8,9,16,128]{3,2,1,0:T(8,128)(2,1)}), bf16[8,9,16,128]{3,2,1,0:T(8,128)(2,1)S(1)}, u32[]{:S(2)}, u32[]{:S(2)}) async-start(bf16[8,9,16,128]{3,2,1,0:T(8,128)(2,1)} %bitcast.22), calls=%async_computation | async-start | bytes 589824 | tf_op jit(solution)/shard_map/all_to_all | solution.py:457
  11.2 3.3 %collective-permute-start = (f32[9,16,128]{2,1,0:T(8,128)S(1)}, f32[9,16,128]{2,1,0:T(8,128)S(1)}, u32[]{:S(2)}, u32[]{:S(2)}) collective-permute-start(f32[9,16,128]{2,1,0:T(8,128)S(1)} %copy-done.5), channel_id=1, source_target_pairs={{0,1},{1,0},{2,3},{3,2},{4,5},{5,4},{6,7},{7,6},{8,9},{9,8},{10,11... | collective-permute-start | bytes 221192 | tf_op jit(solution)/shard_map/ppermute | solution.py:443
  14.6 4.5 %copy-start.6 = (f32[9,16,128]{2,1,0:T(8,128)}, f32[9,16,128]{2,1,0:T(8,128)S(1)}, u32[]{:S(2)}) copy-start(f32[9,16,128]{2,1,0:T(8,128)S(1)} %collective-permute-done.theirs) | copy-start | bytes 221188
  19.1 0.7 copy-start.3
  21.8 24.7 %collective-permute-start.1 = (bf16[46,32,128]{2,1,0:T(8,128)(2,1)}, bf16[46,32,128]{2,1,0:T(8,128)(2,1)S(1)}, u32[]{:S(2)}, u32[]{:S(2)}) collective-permute-start(bf16[46,32,128]{2,1,0:T(8,128)(2,1)} %get-tuple-element.14.one), channel_id=1, source_target_pairs={{0,8},{8,16},{9,1},{16,24},{17,9},{24,32},{25,17},{32,40},{33,25},... | collective-permute-start | bytes 1130504 | tf_op jit(solution)/shard_map/ppermute | solution.py:440
  26.5 19.9 %collective-permute-start.2 = (bf16[37,32,128]{2,1,0:T(8,128)(2,1)}, bf16[37,32,128]{2,1,0:T(8,128)(2,1)S(1)}, u32[]{:S(2)}, u32[]{:S(2)}) collective-permute-start(bf16[37,32,128]{2,1,0:T(8,128)(2,1)} %get-tuple-element.15), channel_id=1, source_target_pairs={{0,16},{8,24},{16,32},{17,1},{24,40},{25,9},{32,48},{33,17},{40,56... | collective-permute-start | bytes 909320 | tf_op jit(solution)/shard_map/ppermute | solution.py:440
  33.5 13.0 %collective-permute-start.3 = (bf16[14,32,128]{2,1,0:T(8,128)(2,1)}, bf16[14,32,128]{2,1,0:T(8,128)(2,1)S(1)}, u32[]{:S(2)}, u32[]{:S(2)}) collective-permute-start(bf16[14,32,128]{2,1,0:T(8,128)(2,1)} %get-tuple-element.16), channel_id=1, source_target_pairs={{0,24},{8,32},{16,40},{24,48},{25,1},{32,56},{33,9},{40,64},{41,17... | collective-permute-start | bytes 344072 | tf_op jit(solution)/shard_map/ppermute | solution.py:440
  46.5 0.7 copy-start.4
  46.5 0.8 copy-start.2
  46.5 0.9 copy-start
  47.4 4.2 %collective-permute-start.4 = (bf16[97,32,128]{2,1,0:T(8,128)(2,1)S(1)}, bf16[97,32,128]{2,1,0:T(8,128)(2,1)S(1)}, u32[]{:S(2)}, u32[]{:S(2)}) collective-permute-start(bf16[97,32,128]{2,1,0:T(8,128)(2,1)S(1)} %pad_maximum_fusion), channel_id=1, source_target_pairs={{0,1},{1,0},{2,3},{3,2},{4,5},{5,4},{6,7},{7,6},{8,9},{9,8},{10,11... | collective-permute-start | bytes 2383880 | tf_op jit(solution)/shard_map/ppermute | solution.py:443
  51.6 0.9 copy-start.1
  63.3 12.9 %collective-permute-start.6 = (f32[7,32,128]{2,1,0:T(8,128)}, f32[7,32,128]{2,1,0:T(8,128)S(1)}, u32[]{:S(2)}, u32[]{:S(2)}) collective-permute-start(f32[7,32,128]{2,1,0:T(8,128)} %get-tuple-element.17.rest_0_), channel_id=1, source_target_pairs={{0,16},{8,24},{16,32},{17,1},{24,40},{25,9},{32,48},{33,17},{40,56... | collective-permute-start | bytes 344072 | tf_op jit(solution)/shard_map/ppermute | solution.py:440
  71.4 7.4 %collective-permute-start.5 = (f32[7,32,128]{2,1,0:T(8,128)}, f32[7,32,128]{2,1,0:T(8,128)S(1)}, u32[]{:S(2)}, u32[]{:S(2)}) collective-permute-start(f32[7,32,128]{2,1,0:T(8,128)} %get-tuple-element.17.rest_0_), channel_id=1, source_target_pairs={{0,8},{8,16},{9,1},{16,24},{17,9},{24,32},{25,17},{32,40},{33,25},... | collective-permute-start | bytes 344072 | tf_op jit(solution)/shard_map/ppermute | solution.py:440
  76.2 2.7 %copy-start.7 = (f32[7,32,128]{2,1,0:T(8,128)}, f32[7,32,128]{2,1,0:T(8,128)S(1)}, u32[]{:S(2)}) copy-start(f32[7,32,128]{2,1,0:T(8,128)S(1)} %collective-permute-done.6.rest_2_) | copy-start | bytes 344068
  78.8 0.7 copy-start.8
  79.5 3.4 %collective-permute-start.7 = (f32[14,32,128]{2,1,0:T(8,128)S(1)}, f32[14,32,128]{2,1,0:T(8,128)S(1)}, u32[]{:S(2)}, u32[]{:S(2)}) collective-permute-start(f32[14,32,128]{2,1,0:T(8,128)S(1)} %pad_maximum_fusion.1), channel_id=1, source_target_pairs={{0,1},{1,0},{2,3},{3,2},{4,5},{5,4},{6,7},{7,6},{8,9},{9,8},{10,11... | collective-permute-start | bytes 688136 | tf_op jit(solution)/shard_map/ppermute | solution.py:443
  82.9 0.7 copy-start.9
  113.5 33.0 %copy-start.12 = (f32[3,2,16,128]{3,2,1,0:T(8,128)S(1)}, f32[3,2,16,128]{3,2,1,0:T(8,128)}, u32[]{:S(2)}) copy-start(f32[3,2,16,128]{3,2,1,0:T(8,128)} %get-tuple-element.19) | copy-start | bytes 147460
  114.1 54.9 %all-to-all-start.2 = ((f32[8,8,128]{2,1,0:T(8,128)}), f32[8,8,128]{2,1,0:T(8,128)S(1)}, u32[]{:S(2)}, u32[]{:S(2)}) async-start(f32[8,8,128]{2,1,0:T(8,128)} %broadcast_in_dim.7), calls=%async_computation.2 | async-start | bytes 65536 | tf_op jit(solution)/shard_map/all_to_all | solution.py:500

commit v2 on v1

--- a/solution.py
+++ b/solution.py
@@ -48,17 +48,29 @@
     return jnp.where((lane < width) | (lane >= LANES - width), back, 0.0)
 
 
-def outgoing(cols, ckpt, obs, mask, drag, send, coded):
-    segs, rows, levels = obs.shape[0], obs.shape[1], obs.shape[2]
+def outgoing(cols, drag, ckpt, obs, mask, send, coded, wide):
+    segs, rows = obs.shape[0], 2
+    levels = obs.shape[1] // rows
     lane = lane_ids((levels, LANES))
     low = lane < LANES // 2
+    for comp in range(3):
+        wide[comp] = ckpt[comp].astype(F32)
+
+    def plane(comp, r, c):
+        return wide[comp, pl.ds(c * rows + r, levels, stride=rows * cols), :]
+
     observed = []
     for s in range(segs):
         for r in range(rows):
-            value = jnp.where(mask[s, r] > 0, obs[s, r], UNSEEN)
+            spot = pl.ds(r, levels, stride=rows)
+            value = jnp.where(mask[s, spot, :] > 0, obs[s, spot, :], UNSEEN)
             coded[s * rows + r] = value
             observed.append(value)
-    coded[segs * rows] = jnp.broadcast_to(drag[...], (levels, LANES))
+    level = lax.broadcasted_iota(jnp.int32, (levels, LANES), 0)
+    rates = jnp.zeros((levels, LANES), F32)
+    for k in range(levels):
+        rates = jnp.where(level == k, drag[k], rates)
+    coded[segs * rows] = rates
     obs_tiles = []
     for pair in (SEGS[:2], SEGS[2:]):
         strips = []
@@ -71,15 +83,11 @@
         strips = []
         for comp in range(3):
             for r in range(rows):
-                own = ckpt[comp, r, :, c * LANES : (c + 1) * LANES]
+                own = plane(comp, r, c).astype(BF)
                 for z in range(2):
                     send[c, z, comp * rows + r] = own
-                left = ckpt[comp, r, :, (c - 1) * LANES : c * LANES].astype(F32) if c else zero
-                right = (
-                    ckpt[comp, r, :, (c + 1) * LANES : (c + 2) * LANES].astype(F32)
-                    if c < cols - 1
-                    else zero
-                )
+                left = plane(comp, r, c - 1) if c else zero
+                right = plane(comp, r, c + 1) if c < cols - 1 else zero
                 strips.append(jnp.where(low, right, left))
         tiles = [pack(strips, HALO).astype(BF)] + obs_tiles
         for t, tile in enumerate(tiles):
@@ -445,13 +453,15 @@
     send, coded = call(
         functools.partial(outgoing, cols),
         (sds((cols, cores, 9, levels, LANES), BF), sds((segs * rows + 1, levels, LANES))),
-        (),
+        (drag,),
         (
-            checkpoints[0].transpose(0, 2, 1, 3),
-            obs_values.transpose(0, 2, 1, 3),
-            obs_mask.transpose(0, 2, 1, 3),
-            drag[:, None],
+            checkpoints.reshape(3, levels, rows, cols, lanes)
+            .transpose(0, 1, 3, 2, 4)
+            .reshape(3, levels * cols * rows, lanes),
+            obs_values.reshape(segs, levels * rows, lanes),
+            obs_mask.reshape(segs, levels * rows, lanes),
         ),
+        [pltpu.VMEM((3, levels * cols * rows, LANES), F32)],
     )
     theirs = swap(coded)
     got = lax.all_to_all(
@@ -463,8 +473,10 @@
         tuple(sds((n, full, LANES), BF) for n in REACH),
         (place,),
         (got, coded, theirs),
-    )
-    came = [toward(block, d + 1) for d, block in enumerate(ones)]
+        (),
+        4 << 20,
+    )
+    came = [toward(block, 3 - d) for d, block in enumerate(ones[::-1])][::-1]
     swapped = swap(jnp.concatenate(came))
 
     def scratch():
@@ -484,6 +496,7 @@
         (place,),
         data,
         scratch(),
+        14 << 20,
     )
     near, next_ = toward(lam, 1), toward(lam, 2)
     lswap = swap(jnp.concatenate([near, next_]))
@@ -494,10 +507,10 @@
         (place,),
         data + (lam, near, next_, lswap, sums),
         scratch(),
+        14 << 20,
     )
     near_sum = jnp.sum(lax.all_to_all(message, ("gxi", "col"), 0, 0, tiled=True), axis=0)
-    spread = jnp.broadcast_to(near_sum, (outer,) + near_sum.shape)
-    total = jnp.sum(lax.all_to_all(spread, "gxo", 0, 0, tiled=True), axis=0)[0]
+    total = lax.psum(near_sum, "gxo")[0]
     return grad.transpose(0, 2, 1, 3), total[:levels], total[levels : 2 * levels]
 
 

time: 170 us -> 152 us (0.89)
  blocking collectives: 18.8 us -> 49.4 us
  starting transfers between devices: 78.2 us -> 56.5 us
  waiting for transfers between devices: 35.6 us -> 21.3 us
  local copies, waits for them, and re-layouts: 9.65 us -> 1.24 us
  Pallas kernels: 25.7 us -> 21.5 us
    psum x0 -> x1, blocking collectives: none -> 49.4 us  [on_device(): total = lax.psum(near_sum, 'gxo')[0]]
    all_to_all x1, starting transfers between devices: 32.4 us -> 10.6 us  [on_device(): lax.all_to_all(message, ('gxi', 'col'), 0, 0, tiled=True)]
    all_to_all x1 -> x0, blocking collectives: 18.8 us -> none  [on_device(): lax.all_to_all(message, ('gxi', 'col'), 0, 0, tiled=True)]
    all_to_all x1, waiting for transfers between devices: 21.9 us -> 7.55 us  [on_device(): lax.all_to_all(message, ('gxi', 'col'), 0, 0, tiled=True)]
    unnamed x32 -> x3, local copies, waits for them, and re-layouts: 7.78 us -> 0.65 us
    pallas_call x4, Pallas kernels: 25.7 us -> 21.5 us  [call(): pl.pallas_call(kernel, out_shape=outs, in_specs=[smem()] * len(places) +...]
  transfers between devices with their start and end apart: 10 -> 10, of which waited for: 7 -> 7; matrix products, arithmetic and copies ran while one was open for 1% -> 0% of each run, Pallas kernels for 0% -> 0%
where the time goes in v2:
time: 152 us; the launch traced here: 151 us
  starting transfers between devices  56.5 us (37%)
  blocking collectives  49.4 us (32%)
  Pallas kernels  21.5 us (14%)
  waiting for transfers between devices  21.3 us (14%)
    psum x1, blocking collectives, on_device(): total = lax.psum(near_sum, 'gxo')[0]  49.4 us
    ppermute x5, starting transfers between devices, toward(): return lax.ppermute(block, ('gxo', 'gxi', 'gz'), route)  34.9 us
    pallas_call x4, Pallas kernels, call(): pl.pallas_call(kernel, out_shape=outs, in_specs=[smem()] * len(places) +...  21.5 us
    all_to_all x1, starting transfers between devices, on_device(): lax.all_to_all(message, ('gxi', 'col'), 0, 0, tiled=True)  10.6 us
    all_to_all x1, waiting for transfers between devices, on_device(): lax.all_to_all(message, ('gxi', 'col'), 0, 0, tiled=True)  7.55 us
    ppermute x3, starting transfers between devices, swap(): return lax.ppermute(block, 'gz', [(0, 1), (1, 0)])  6.33 us
    all_to_all x1, starting transfers between devices, on_device(): lax.all_to_all(send.reshape(cols * cores, 9, levels, LANES), ('col', 'gz'...  4.72 us
    ppermute x5, waiting for transfers between devices, toward(): return lax.ppermute(block, ('gxo', 'gxi', 'gz'), route)  4.68 us
  transfers between devices with their start and end apart: 10, of which 7 were waited for; matrix products, arithmetic and copies ran while one was open for 0% of the time, Pallas kernels for 0%

profile of v2, /device:TPU:40, one launch (start us, length us, event | category | flops | bytes accessed | tf_op | source)
XLA Modules:
  0.0 151.0 jit_solution(13651917808906525430)
XLA Ops:
  0.6 1.8 %shard_map.67 = (bf16[4,2,9,16,128]{4,3,2,1,0:T(8,128)(2,1)}, f32[9,16,128]{2,1,0:T(8,128)}) custom-call(f32[16]{0:T(128)} %drag.1, bf16[3,128,128]{2,1,0:T(8,128)(2,1)} %bitcast.18, f32[4,32,128]{2,1,0:T(8,128)} %bitcast.19, s32[4,32,128]{2,1,0:T(8,128)} %bitcast.20), custom_call_target="tpu_custom_call" | custom-call | tf_op jit(solution)/shard_map/pallas_call | solution.py:419
  2.4 0.0 copy-start
  2.4 4.7 %all-to-all-start = ((bf16[8,9,16,128]{3,2,1,0:T(8,128)(2,1)}), bf16[8,9,16,128]{3,2,1,0:T(8,128)(2,1)S(1)}, u32[]{:S(2)}, u32[]{:S(2)}) async-start(bf16[8,9,16,128]{3,2,1,0:T(8,128)(2,1)} %bitcast.17), calls=%async_computation | async-start | bytes 589824 | tf_op jit(solution)/shard_map/all_to_all | solution.py:467
  7.2 0.0 copy-done
  7.2 2.4 %collective-permute-start = (f32[9,16,128]{2,1,0:T(8,128)S(1)}, f32[9,16,128]{2,1,0:T(8,128)S(1)}, u32[]{:S(2)}, u32[]{:S(2)}) collective-permute-start(f32[9,16,128]{2,1,0:T(8,128)S(1)} %copy-done), channel_id=1, source_target_pairs={{0,1},{1,0},{2,3},{3,2},{4,5},{5,4},{6,7},{7,6},{8,9},{9,8},{10,11... | collective-permute-start | bytes 221192 | tf_op jit(solution)/shard_map/ppermute | solution.py:451
  9.6 0.1 pad_add_fusion.place
  9.7 0.8 collective-permute-done.theirs
  10.5 4.5 %all-to-all-done.got = bf16[8,9,16,128]{3,2,1,0:T(8,128)(2,1)S(1)} async-done(((bf16[8,9,16,128]{3,2,1,0:T(8,128)(2,1)}), bf16[8,9,16,128]{3,2,1,0:T(8,128)(2,1)S(1)}, u32[]{:S(2)}, u32[]{:S(2)}) %all-to-all-start) | async-done | bytes 294944 | tf_op jit(solution)/shard_map/all_to_all | solution.py:467
  15.0 0.6 shard_map.68
  15.7 4.7 %collective-permute-start.1 = (bf16[46,32,128]{2,1,0:T(8,128)(2,1)S(1)}, bf16[46,32,128]{2,1,0:T(8,128)(2,1)S(1)}, u32[]{:S(2)}, u32[]{:S(2)}) collective-permute-start(bf16[46,32,128]{2,1,0:T(8,128)(2,1)S(1)} %get-tuple-element.14.one), channel_id=1, source_target_pairs={{0,8},{8,16},{9,1},{16,24},{17,9},{24,32},{25,17},{32,40},{33,25},... | collective-permute-start | bytes 1130504 | tf_op jit(solution)/shard_map/ppermute | solution.py:448
  20.4 6.9 %collective-permute-start.2 = (bf16[37,32,128]{2,1,0:T(8,128)(2,1)S(1)}, bf16[37,32,128]{2,1,0:T(8,128)(2,1)S(1)}, u32[]{:S(2)}, u32[]{:S(2)}) collective-permute-start(bf16[37,32,128]{2,1,0:T(8,128)(2,1)S(1)} %get-tuple-element.15), channel_id=1, source_target_pairs={{0,16},{8,24},{16,32},{17,1},{24,40},{25,9},{32,48},{33,17},{40,56... | collective-permute-start | bytes 909320 | tf_op jit(solution)/shard_map/ppermute | solution.py:448
  27.3 10.3 %collective-permute-start.3 = (bf16[14,32,128]{2,1,0:T(8,128)(2,1)S(1)}, bf16[14,32,128]{2,1,0:T(8,128)(2,1)S(1)}, u32[]{:S(2)}, u32[]{:S(2)}) collective-permute-start(bf16[14,32,128]{2,1,0:T(8,128)(2,1)S(1)} %get-tuple-element.16), channel_id=1, source_target_pairs={{0,24},{8,32},{16,40},{24,48},{25,1},{32,56},{33,9},{40,64},{41,17... | collective-permute-start | bytes 344072 | tf_op jit(solution)/shard_map/ppermute | solution.py:448
  37.7 2.3 %collective-permute-done.3.r3 = bf16[14,32,128]{2,1,0:T(8,128)(2,1)S(1)} collective-permute-done((bf16[14,32,128]{2,1,0:T(8,128)(2,1)S(1)}, bf16[14,32,128]{2,1,0:T(8,128)(2,1)S(1)}, u32[]{:S(2)}, u32[]{:S(2)}) %collective-permute-start.3) | collective-permute-done | bytes 114720 | tf_op jit(solution)/shard_map/ppermute | solution.py:448
  40.0 0.0 collective-permute-done.2.r2
  40.0 0.0 collective-permute-done.1.r1
  40.0 0.1 pad_maximum_fusion
  40.1 2.0 %collective-permute-start.4 = (bf16[97,32,128]{2,1,0:T(8,128)(2,1)S(1)}, bf16[97,32,128]{2,1,0:T(8,128)(2,1)S(1)}, u32[]{:S(2)}, u32[]{:S(2)}) collective-permute-start(bf16[97,32,128]{2,1,0:T(8,128)(2,1)S(1)} %pad_maximum_fusion), channel_id=1, source_target_pairs={{0,1},{1,0},{2,3},{3,2},{4,5},{5,4},{6,7},{7,6},{8,9},{9,8},{10,11... | collective-permute-start | bytes 2383880 | tf_op jit(solution)/shard_map/ppermute | solution.py:451
  42.1 2.3 %collective-permute-done.4.swapped = bf16[97,32,128]{2,1,0:T(8,128)(2,1)S(1)} collective-permute-done((bf16[97,32,128]{2,1,0:T(8,128)(2,1)S(1)}, bf16[97,32,128]{2,1,0:T(8,128)(2,1)S(1)}, u32[]{:S(2)}, u32[]{:S(2)}) %collective-permute-start.4) | collective-permute-done | bytes 794656 | tf_op jit(solution)/shard_map/ppermute | solution.py:451
  44.4 9.2 %shard_map.69 = (f32[7,32,128]{2,1,0:T(8,128)S(1)}, f32[2,32,128]{2,1,0:T(8,128)S(1)}) custom-call(s32[3]{0:T(128)S(1)} %pad_add_fusion.place, f32[9,16,128]{2,1,0:T(8,128)S(1)} %copy-done, f32[9,16,128]{2,1,0:T(8,128)S(1)} %collective-permute-done.theirs, bf16[46,32,128]{2,1,0:T(8,128)(2,1)S(1)} %get-tuple-element.14.one, ...), custom_call_target="tpu_custom_call" | custom-call | tf_op jit(solution)/shard_map/pallas_call | solution.py:419
  53.5 8.1 %collective-permute-start.6 = (f32[7,32,128]{2,1,0:T(8,128)S(1)}, f32[7,32,128]{2,1,0:T(8,128)S(1)}, u32[]{:S(2)}, u32[]{:S(2)}) collective-permute-start(f32[7,32,128]{2,1,0:T(8,128)S(1)} %get-tuple-element.17.rest_0_), channel_id=1, source_target_pairs={{0,16},{8,24},{16,32},{17,1},{24,40},{25,9},{32,48},{33,17},{40,56... | collective-permute-start | bytes 344072 | tf_op jit(solution)/shard_map/ppermute | solution.py:448
  61.7 4.7 %collective-permute-start.5 = (f32[7,32,128]{2,1,0:T(8,128)S(1)}, f32[7,32,128]{2,1,0:T(8,128)S(1)}, u32[]{:S(2)}, u32[]{:S(2)}) collective-permute-start(f32[7,32,128]{2,1,0:T(8,128)S(1)} %get-tuple-element.17.rest_0_), channel_id=1, source_target_pairs={{0,8},{8,16},{9,1},{16,24},{17,9},{24,32},{25,17},{32,40},{33,25},... | collective-permute-start | bytes 344072 | tf_op jit(solution)/shard_map/ppermute | solution.py:448
  66.4 0.0 collective-permute-done.6.rest_2_
  66.4 2.3 %collective-permute-done.5.rest_1_ = f32[7,32,128]{2,1,0:T(8,128)S(1)} collective-permute-done((f32[7,32,128]{2,1,0:T(8,128)S(1)}, f32[7,32,128]{2,1,0:T(8,128)S(1)}, u32[]{:S(2)}, u32[]{:S(2)}) %collective-permute-start.5) | collective-permute-done | bytes 114720 | tf_op jit(solution)/shard_map/ppermute | solution.py:448
  68.8 2.0 %collective-permute-start.7 = (f32[14,32,128]{2,1,0:T(8,128)S(1)}, f32[14,32,128]{2,1,0:T(8,128)S(1)}, u32[]{:S(2)}, u32[]{:S(2)}) collective-permute-start(f32[14,32,128]{2,1,0:T(8,128)S(1)} %pad_maximum_fusion.1), channel_id=1, source_target_pairs={{0,1},{1,0},{2,3},{3,2},{4,5},{5,4},{6,7},{7,6},{8,9},{9,8},{10,11... | collective-permute-start | bytes 688136 | tf_op jit(solution)/shard_map/ppermute | solution.py:451
  70.7 1.5 collective-permute-done.7.rest_3_
  72.2 9.9 %shard_map.70 = (f32[3,2,16,128]{3,2,1,0:T(8,128)S(1)}, f32[16,8,128]{2,1,0:T(8,128)}) custom-call(s32[3]{0:T(128)S(1)} %pad_add_fusion.place, f32[9,16,128]{2,1,0:T(8,128)S(1)} %copy-done, f32[9,16,128]{2,1,0:T(8,128)S(1)} %collective-permute-done.theirs, bf16[46,32,128]{2,1,0:T(8,128)(2,1)S(1)} %get-tuple-element.14.one, ...), custom_call_target="tpu_custom_call" | custom-call | tf_op jit(solution)/shard_map/pallas_call | solution.py:419
  82.1 10.6 %all-to-all-start.1 = ((f32[16,8,128]{2,1,0:T(8,128)}), f32[16,8,128]{2,1,0:T(8,128)S(1)}, u32[]{:S(2)}, u32[]{:S(2)}) async-start(f32[16,8,128]{2,1,0:T(8,128)} %get-tuple-element.20), calls=%async_computation.1 | async-start | bytes 131072 | tf_op jit(solution)/shard_map/all_to_all | solution.py:512
  92.7 0.6 copy.8
  93.4 7.5 %all-to-all-done.1 = f32[16,8,128]{2,1,0:T(8,128)S(1)} async-done(((f32[16,8,128]{2,1,0:T(8,128)}), f32[16,8,128]{2,1,0:T(8,128)S(1)}, u32[]{:S(2)}, u32[]{:S(2)}) %all-to-all-start.1) | async-done | bytes 65568 | tf_op jit(solution)/shard_map/all_to_all | solution.py:512
  101.0 49.4 %psum.7 = f32[8,128]{1,0:T(8,128)S(1)} all-reduce(f32[8,128]{1,0:T(8,128)S(1)} %reduce_sum.9), channel_id=1, replica_groups=mesh['ens'=2,'gxo'=8,'gxi'=4,'col'=4,'gz'=2] {'gxo'}, use_global_device_ids=true, to_apply=%region_1.0 | all-reduce | flops 1024 | bytes 8192 | tf_op jit(solution)/shard_map/psum | solution.py:513
  150.4 0.6 slice_bitcast_fusion
  (2 shorter events, 0.0 us)
Async XLA Ops:
  2.4 4.7 %copy-start = (f32[9,16,128]{2,1,0:T(8,128)S(1)}, f32[9,16,128]{2,1,0:T(8,128)}, u32[]{:S(2)}) copy-start(f32[9,16,128]{2,1,0:T(8,128)} %get-tuple-element.12.coded) | copy-start | bytes 221188
  2.4 12.6 %all-to-all-start = ((bf16[8,9,16,128]{3,2,1,0:T(8,128)(2,1)}), bf16[8,9,16,128]{3,2,1,0:T(8,128)(2,1)S(1)}, u32[]{:S(2)}, u32[]{:S(2)}) async-start(bf16[8,9,16,128]{3,2,1,0:T(8,128)(2,1)} %bitcast.17), calls=%async_computation | async-start | bytes 589824 | tf_op jit(solution)/shard_map/all_to_all | solution.py:467
  7.2 3.3 %collective-permute-start = (f32[9,16,128]{2,1,0:T(8,128)S(1)}, f32[9,16,128]{2,1,0:T(8,128)S(1)}, u32[]{:S(2)}, u32[]{:S(2)}) collective-permute-start(f32[9,16,128]{2,1,0:T(8,128)S(1)} %copy-done), channel_id=1, source_target_pairs={{0,1},{1,0},{2,3},{3,2},{4,5},{5,4},{6,7},{7,6},{8,9},{9,8},{10,11... | collective-permute-start | bytes 221192 | tf_op jit(solution)/shard_map/ppermute | solution.py:451
  15.7 24.4 %collective-permute-start.1 = (bf16[46,32,128]{2,1,0:T(8,128)(2,1)S(1)}, bf16[46,32,128]{2,1,0:T(8,128)(2,1)S(1)}, u32[]{:S(2)}, u32[]{:S(2)}) collective-permute-start(bf16[46,32,128]{2,1,0:T(8,128)(2,1)S(1)} %get-tuple-element.14.one), channel_id=1, source_target_pairs={{0,8},{8,16},{9,1},{16,24},{17,9},{24,32},{25,17},{32,40},{33,25},... | collective-permute-start | bytes 1130504 | tf_op jit(solution)/shard_map/ppermute | solution.py:448
  20.4 19.6 %collective-permute-start.2 = (bf16[37,32,128]{2,1,0:T(8,128)(2,1)S(1)}, bf16[37,32,128]{2,1,0:T(8,128)(2,1)S(1)}, u32[]{:S(2)}, u32[]{:S(2)}) collective-permute-start(bf16[37,32,128]{2,1,0:T(8,128)(2,1)S(1)} %get-tuple-element.15), channel_id=1, source_target_pairs={{0,16},{8,24},{16,32},{17,1},{24,40},{25,9},{32,48},{33,17},{40,56... | collective-permute-start | bytes 909320 | tf_op jit(solution)/shard_map/ppermute | solution.py:448
  27.3 12.7 %collective-permute-start.3 = (bf16[14,32,128]{2,1,0:T(8,128)(2,1)S(1)}, bf16[14,32,128]{2,1,0:T(8,128)(2,1)S(1)}, u32[]{:S(2)}, u32[]{:S(2)}) collective-permute-start(bf16[14,32,128]{2,1,0:T(8,128)(2,1)S(1)} %get-tuple-element.16), channel_id=1, source_target_pairs={{0,24},{8,32},{16,40},{24,48},{25,1},{32,56},{33,9},{40,64},{41,17... | collective-permute-start | bytes 344072 | tf_op jit(solution)/shard_map/ppermute | solution.py:448
  40.1 4.2 %collective-permute-start.4 = (bf16[97,32,128]{2,1,0:T(8,128)(2,1)S(1)}, bf16[97,32,128]{2,1,0:T(8,128)(2,1)S(1)}, u32[]{:S(2)}, u32[]{:S(2)}) collective-permute-start(bf16[97,32,128]{2,1,0:T(8,128)(2,1)S(1)} %pad_maximum_fusion), channel_id=1, source_target_pairs={{0,1},{1,0},{2,3},{3,2},{4,5},{5,4},{6,7},{7,6},{8,9},{9,8},{10,11... | collective-permute-start | bytes 2383880 | tf_op jit(solution)/shard_map/ppermute | solution.py:451
  53.5 12.9 %collective-permute-start.6 = (f32[7,32,128]{2,1,0:T(8,128)S(1)}, f32[7,32,128]{2,1,0:T(8,128)S(1)}, u32[]{:S(2)}, u32[]{:S(2)}) collective-permute-start(f32[7,32,128]{2,1,0:T(8,128)S(1)} %get-tuple-element.17.rest_0_), channel_id=1, source_target_pairs={{0,16},{8,24},{16,32},{17,1},{24,40},{25,9},{32,48},{33,17},{40,56... | collective-permute-start | bytes 344072 | tf_op jit(solution)/shard_map/ppermute | solution.py:448
  61.7 7.1 %collective-permute-start.5 = (f32[7,32,128]{2,1,0:T(8,128)S(1)}, f32[7,32,128]{2,1,0:T(8,128)S(1)}, u32[]{:S(2)}, u32[]{:S(2)}) collective-permute-start(f32[7,32,128]{2,1,0:T(8,128)S(1)} %get-tuple-element.17.rest_0_), channel_id=1, source_target_pairs={{0,8},{8,16},{9,1},{16,24},{17,9},{24,32},{25,17},{32,40},{33,25},... | collective-permute-start | bytes 344072 | tf_op jit(solution)/shard_map/ppermute | solution.py:448
  68.8 3.4 %collective-permute-start.7 = (f32[14,32,128]{2,1,0:T(8,128)S(1)}, f32[14,32,128]{2,1,0:T(8,128)S(1)}, u32[]{:S(2)}, u32[]{:S(2)}) collective-permute-start(f32[14,32,128]{2,1,0:T(8,128)S(1)} %pad_maximum_fusion.1), channel_id=1, source_target_pairs={{0,1},{1,0},{2,3},{3,2},{4,5},{5,4},{6,7},{7,6},{8,9},{9,8},{10,11... | collective-permute-start | bytes 688136 | tf_op jit(solution)/shard_map/ppermute | solution.py:451
  82.1 18.8 %all-to-all-start.1 = ((f32[16,8,128]{2,1,0:T(8,128)}), f32[16,8,128]{2,1,0:T(8,128)S(1)}, u32[]{:S(2)}, u32[]{:S(2)}) async-start(f32[16,8,128]{2,1,0:T(8,128)} %get-tuple-element.20), calls=%async_computation.1 | async-start | bytes 131072 | tf_op jit(solution)/shard_map/all_to_all | solution.py:512
